TPU v7x, 256 devices: a whole 4x4x8 slice. The times are simulated.
256 devices in a mesh: strip: 256 (over x, z, y, core).
Axes of the slice: x: 4, y: 4, z: 8, core: 2. Of those that a mesh axis runs over, the one named last changes fastest.
Arguments:
- features: bfloat16 [64, 8192, 1024], P(None, 'strip'), may hold values from -6 to 6
- row_kernel: bfloat16 [8, 8, 8, 129], replicated, may hold values from -0.1875 to 0.1875
- mix_weight: bfloat16 [64, 64], replicated, may hold values from -0.75 to 0.75
- channel_bias: float32 [64], replicated, may hold values from -3 to 3
Outputs:
- layer_out: bfloat16 [64, 8192, 1024], P(None, 'strip')
All inputs are finite; a program needn't handle non-finite values.
Results may differ from a plain program's by a relative error of at most 0.001.
Values may be sent and summed in bfloat16 or wider, within the bound.
No kernel may reach another device: no remote copies, remote signals or barrier semaphores. Data moves between devices by JAX's collectives and lax.ppermute only.
A program may use at most 128 MiB of HBM per device.

v0:
```python
import jax
import jax.numpy as jnp
from jax import lax
from jax.sharding import PartitionSpec as P


def passed_along(block, axis, distance):
    devices = range(lax.axis_size(axis))
    route = [((i - distance) % len(devices), i) for i in devices]
    return lax.ppermute(block, axis, route)


def local(features, row_kernel, mix_weight, channel_bias):
    channels, strip_rows, columns = features.shape
    group_count, group_width, _, tap_count = row_kernel.shape
    reach = (tap_count - 1) // 2
    strips_away = reach // strip_rows
    above_list = [
        passed_along(features, "strip", distance) for distance in range(strips_away, 0, -1)
    ]
    below_list = [
        passed_along(features, "strip", -distance) for distance in range(1, strips_away + 1)
    ]
    above = jnp.concatenate(above_list, axis=1)
    below = jnp.concatenate(below_list, axis=1)
    ext_rows = strip_rows + 2 * reach
    out_index = lax.broadcasted_iota(jnp.int32, (strip_rows, ext_rows, tap_count), 0)
    in_index = lax.broadcasted_iota(jnp.int32, (strip_rows, ext_rows, tap_count), 1)
    tap_index = lax.broadcasted_iota(jnp.int32, (strip_rows, ext_rows, tap_count), 2)
    one_hot = (in_index - out_index == tap_index).astype(jnp.float32)
    banded = jnp.einsum("goct,pit->gopci", row_kernel.astype(jnp.float32), one_hot).astype(
        jnp.bfloat16
    )
    out_width = group_width * strip_rows
    joined = jnp.concatenate([above, features, below], axis=1)
    span = joined.shape[1]
    matrix = banded.reshape(group_count, out_width, group_width * span)
    data = joined.reshape(group_count, group_width * span, columns)
    conv = jnp.einsum("gab,gbw->gaw", matrix, data, preferred_element_type=jnp.float32)
    conv = conv.reshape(channels, strip_rows, columns)
    mixed = jnp.einsum("io,irw->orw", mix_weight, features, preferred_element_type=jnp.float32)
    total = conv + mixed + channel_bias[:, None, None]
    return jax.nn.gelu(total).astype(jnp.bfloat16)


def solution(mesh):
    return jax.shard_map(
        local,
        mesh=mesh,
        in_specs=(P(None, "strip", None), P(), P(), P()),
        out_specs=P(None, "strip", None),
        check_vma=False,
    )
```

profile of v0, /device:TPU:0, one launch (start us, length us, event | category | flops | bytes accessed | tf_op | source)
XLA Modules:
  0.0 195.9 jit_solution(12046841574717847914)
XLA Ops:
  0.0 0.0 copy-start
  0.0 0.0 collective-permute-start
  0.0 0.0 collective-permute-start.1
  0.0 8.4 %collective-permute-start.2 = (bf16[64,32,1024]{2,1,0:T(8,128)(2,1)}, bf16[64,32,1024]{2,1,0:T(8,128)(2,1)}, u32[]{:S(2)}, u32[]{:S(2)}) collective-permute-start(bf16[64,32,1024]{2,1,0:T(8,128)(2,1)} %param.4), channel_id=1, source_target_pairs={{1,0},{2,1},{3,2},{4,3},{5,4},{6,5},{7,6},{8,7},{9,8},{10,9},{11,1... | collective-permute-start | bytes 12582920 | tf_op jit(solution)/shard_map/ppermute | solution.py:10
  8.4 2.2 %collective-permute-start.3 = (bf16[64,32,1024]{2,1,0:T(8,128)(2,1)}, bf16[64,32,1024]{2,1,0:T(8,128)(2,1)}, u32[]{:S(2)}, u32[]{:S(2)}) collective-permute-start(bf16[64,32,1024]{2,1,0:T(8,128)(2,1)} %param.4), channel_id=1, source_target_pairs={{2,0},{3,1},{4,2},{5,3},{6,4},{7,5},{8,6},{9,7},{10,8},{11,9},{12,... | collective-permute-start | bytes 12582920 | tf_op jit(solution)/shard_map/ppermute | solution.py:10
  10.6 0.0 copy-done
  10.6 5.6 %convert_bitcast_fusion = bf16[8,8,32,8,160]{4,3,1,0,2:T(8,128)(2,1)} fusion(bf16[8,8,8,129]{3,2,1,0:T(8,128)(2,1)S(1)} %copy-done), kind=kOutput, calls=%fused_computation.11 | convolution fusion | flops 680273920 | bytes 5374976 | tf_op jit(solution)/shard_map/goct,pit->gopci/dot_general | solution.py:31
  16.3 7.7 %copy.9 = bf16[8,8,32,8,160]{4,3,2,1,0:T(8,128)(2,1)} copy(bf16[8,8,32,8,160]{4,3,1,0,2:T(8,128)(2,1)} %convert_bitcast_fusion) | data formatting | bytes 10485760 | tf_op jit(solution)/shard_map/convert_element_type | solution.py:31
  24.0 14.2 %reshape.10 = bf16[8,256,1280]{2,1,0:T(8,128)(2,1)} reshape(bf16[8,8,32,8,160]{4,3,2,1,0:T(8,128)(2,1)} %copy.9) | data formatting | bytes 10485760 | tf_op jit(solution)/shard_map/reshape | solution.py:37
  38.2 62.4 %collective-permute-done = bf16[64,32,1024]{2,1,0:T(8,128)(2,1)} collective-permute-done((bf16[64,32,1024]{2,1,0:T(8,128)(2,1)}, bf16[64,32,1024]{2,1,0:T(8,128)(2,1)}, u32[]{:S(2)}, u32[]{:S(2)}) %collective-permute-start) | collective-permute-done | bytes 4194336 | tf_op jit(solution)/shard_map/ppermute | solution.py:10
  100.5 5.0 %constant_dynamic-update-slice_fusion.4 = bf16[64,160,1024]{2,1,0:T(8,128)(2,1)} fusion(bf16[64,32,1024]{2,1,0:T(8,128)(2,1)} %collective-permute-done), kind=kLoop, calls=%fused_computation.22 | loop fusion | bytes 8388608
  105.6 39.1 %collective-permute-done.1 = bf16[64,32,1024]{2,1,0:T(8,128)(2,1)} collective-permute-done((bf16[64,32,1024]{2,1,0:T(8,128)(2,1)}, bf16[64,32,1024]{2,1,0:T(8,128)(2,1)}, u32[]{:S(2)}, u32[]{:S(2)}) %collective-permute-start.1) | collective-permute-done | bytes 4194336 | tf_op jit(solution)/shard_map/ppermute | solution.py:10
  144.6 5.2 %constant_dynamic-update-slice_fusion.3 = bf16[64,160,1024]{2,1,0:T(8,128)(2,1)} fusion(bf16[64,160,1024]{2,1,0:T(8,128)(2,1)} %constant_dynamic-update-slice_fusion.4, bf16[64,32,1024]{2,1,0:T(8,128)(2,1)} %collective-permute-done.1), kind=kLoop, calls=%fused_computation.21 | loop fusion | bytes 8388608
  149.8 0.0 copy-done.2
  149.8 2.4 %constant_dynamic-update-slice_fusion.2 = bf16[64,160,1024]{2,1,0:T(8,128)(2,1)} fusion(bf16[64,160,1024]{2,1,0:T(8,128)(2,1)} %constant_dynamic-update-slice_fusion.3, bf16[64,32,1024]{2,1,0:T(8,128)(2,1)S(1)} %copy-done.2), kind=kLoop, calls=%fused_computation.20 | loop fusion | bytes 8388608
  152.2 0.0 collective-permute-done.2
  152.2 5.2 %constant_dynamic-update-slice_fusion.1 = bf16[64,160,1024]{2,1,0:T(8,128)(2,1)} fusion(bf16[64,160,1024]{2,1,0:T(8,128)(2,1)} %constant_dynamic-update-slice_fusion.2, bf16[64,32,1024]{2,1,0:T(8,128)(2,1)} %collective-permute-done.2), kind=kLoop, calls=%fused_computation.19 | loop fusion | bytes 8388608
  157.5 0.0 collective-permute-done.3
  157.5 5.2 %constant_dynamic-update-slice_fusion = bf16[64,160,1024]{2,1,0:T(8,128)(2,1)} fusion(bf16[64,160,1024]{2,1,0:T(8,128)(2,1)} %constant_dynamic-update-slice_fusion.1, bf16[64,32,1024]{2,1,0:T(8,128)(2,1)} %collective-permute-done.3), kind=kLoop, calls=%fused_computation.18 | loop fusion | bytes 8388608 | tf_op jit(solution)/shard_map/concatenate | solution.py:35
  162.6 0.0 slice-done
  162.6 0.0 copy-start.4
  162.6 15.0 %fusion.17 = f32[8,256,1024]{2,1,0:T(8,128)} fusion(bf16[8,256,1280]{2,1,0:T(8,128)(2,1)S(1)} %bitcast.20, bf16[8,1280,1024]{2,1,0:T(8,128)(2,1)} %bitcast.4), kind=kOutput, calls=%fused_computation.23 | convolution fusion | flops 5368709120 | bytes 34603008 | tf_op jit(solution)/shard_map/gab,gbw->gaw/dot_general | solution.py:39
  177.6 13.9 %fusion.7 = bf16[64,32,1024]{2,0,1:T(8,128)(2,1)S(1)} fusion(f32[64,32,1024]{2,1,0:T(8,128)} %bitcast.21, f32[64]{0:T(128)S(1)} %copy-done.4, bf16[64,32,1024]{2,1,0:T(8,128)(2,1)S(1)} %copy-done.2, bf16[64,64]{1,0:T(8,128)(2,1)S(1)} %copy-done.3), kind=kOutput, calls=%fused_computation.8 | convolution fusion | flops 291504128 | bytes 16785664 | tf_op jit(solution)/shard_map/io,irw->orw/dot_general | solution.py:41
  191.5 4.3 %copy.13 = bf16[64,32,1024]{2,1,0:T(8,128)(2,1)} copy(bf16[64,32,1024]{2,0,1:T(8,128)(2,1)S(1)} %fusion.7) | data formatting | bytes 8388608 | tf_op jit(solution)/shard_map/convert_element_type | solution.py:43
  (10 shorter events, 0.0 us)
Async XLA Ops:
  0.0 10.6 %copy-start = (bf16[8,8,8,129]{3,2,1,0:T(8,128)(2,1)S(1)}, bf16[8,8,8,129]{3,2,1,0:T(8,128)(2,1)}, u32[]{:S(2)}) copy-start(bf16[8,8,8,129]{3,2,1,0:T(8,128)(2,1)} %param.5) | copy-start | bytes 396292
  0.0 100.5 %collective-permute-start = (bf16[64,32,1024]{2,1,0:T(8,128)(2,1)}, bf16[64,32,1024]{2,1,0:T(8,128)(2,1)}, u32[]{:S(2)}, u32[]{:S(2)}) collective-permute-start(bf16[64,32,1024]{2,1,0:T(8,128)(2,1)} %param.4), channel_id=1, source_target_pairs={{254,0},{255,1},{0,2},{1,3},{2,4},{3,5},{4,6},{5,7},{6,8},{7,9},{8... | collective-permute-start | bytes 12582920 | tf_op jit(solution)/shard_map/ppermute | solution.py:10
  0.0 144.6 %collective-permute-start.1 = (bf16[64,32,1024]{2,1,0:T(8,128)(2,1)}, bf16[64,32,1024]{2,1,0:T(8,128)(2,1)}, u32[]{:S(2)}, u32[]{:S(2)}) collective-permute-start(bf16[64,32,1024]{2,1,0:T(8,128)(2,1)} %param.4), channel_id=1, source_target_pairs={{255,0},{0,1},{1,2},{2,3},{3,4},{4,5},{5,6},{6,7},{7,8},{8,9},{9,1... | collective-permute-start | bytes 12582920 | tf_op jit(solution)/shard_map/ppermute | solution.py:10
  0.0 152.2 %collective-permute-start.2 = (bf16[64,32,1024]{2,1,0:T(8,128)(2,1)}, bf16[64,32,1024]{2,1,0:T(8,128)(2,1)}, u32[]{:S(2)}, u32[]{:S(2)}) collective-permute-start(bf16[64,32,1024]{2,1,0:T(8,128)(2,1)} %param.4), channel_id=1, source_target_pairs={{1,0},{2,1},{3,2},{4,3},{5,4},{6,5},{7,6},{8,7},{9,8},{10,9},{11,1... | collective-permute-start | bytes 12582920 | tf_op jit(solution)/shard_map/ppermute | solution.py:10
  8.4 149.1 %collective-permute-start.3 = (bf16[64,32,1024]{2,1,0:T(8,128)(2,1)}, bf16[64,32,1024]{2,1,0:T(8,128)(2,1)}, u32[]{:S(2)}, u32[]{:S(2)}) collective-permute-start(bf16[64,32,1024]{2,1,0:T(8,128)(2,1)} %param.4), channel_id=1, source_target_pairs={{2,0},{3,1},{4,2},{5,3},{6,4},{7,5},{8,6},{9,7},{10,8},{11,9},{12,... | collective-permute-start | bytes 12582920 | tf_op jit(solution)/shard_map/ppermute | solution.py:10
  38.2 111.6 %copy-start.2 = (bf16[64,32,1024]{2,1,0:T(8,128)(2,1)S(1)}, bf16[64,32,1024]{2,1,0:T(8,128)(2,1)}, u32[]{:S(2)}) copy-start(bf16[64,32,1024]{2,1,0:T(8,128)(2,1)} %param.4) | copy-start | bytes 12582916
  152.2 10.4 %slice-start = ((s8[5242880]{0:T(1024)(128)(4,1)}), s8[4194304]{0:T(1024)(128)(4,1)S(1)}, s32[]{:S(2)}) async-start(s8[5242880]{0:T(1024)(128)(4,1)} %bitcast.19), calls=%async_computation | async-start | bytes 8388608
  157.5 5.2 %slice-start.1 = ((s8[5242880]{0:T(1024)(128)(4,1)}), s8[1048576]{0:T(1024)(128)(4,1)S(1)}, s32[]{:S(2)}) async-start(s8[5242880]{0:T(1024)(128)(4,1)} %bitcast.19), calls=%async_computation.1 | async-start | bytes 2097152
  162.6 15.0 %copy-start.3 = (bf16[64,64]{1,0:T(8,128)(2,1)S(1)}, bf16[64,64]{1,0:T(8,128)(2,1)}, u32[]{:S(2)}) copy-start(bf16[64,64]{1,0:T(8,128)(2,1)} %param.6) | copy-start | bytes 24580
  162.6 15.0 %copy-start.4 = (f32[64]{0:T(128)S(1)}, f32[64]{0:T(128)}, u32[]{:S(2)}) copy-start(f32[64]{0:T(128)} %param.7) | copy-start | bytes 772
  177.6 18.2 %copy-start.1 = (bf16[8,8,8,129]{3,2,1,0:T(8,128)(2,1)S(1)}, bf16[8,8,8,129]{3,2,1,0:T(8,128)(2,1)}, u32[]{:S(2)}) copy-start(bf16[8,8,8,129]{3,2,1,0:T(8,128)(2,1)} %param.5) | copy-start | bytes 396292
where the time goes:
time: 196 us
  waiting for transfers between devices  101 us (52%)
  local copies, waits for them, and re-layouts  49.3 us (25%)
  matrix products  34.5 us (18%)
  starting transfers between devices  10.6 us (5%)
    ppermute x4, waiting for transfers between devices, passed_along(): return lax.ppermute(block, axis, route)  101 us
    unnamed x18, local copies, waits for them, and re-layouts  17.9 us
    dot_general x1, matrix products, local(): jnp.einsum('gab,gbw->gaw', matrix, data, preferred_element_type=jnp.float32)  15 us
    reshape x1, local copies, waits for them, and re-layouts, local(): matrix = banded.reshape(group_count, out_width, group_width * span)  14.2 us
    dot_general x1, matrix products, local(): jnp.einsum('io,irw->orw', mix_weight, features, preferred_element_type=jn...  13.9 us
    ppermute x4, starting transfers between devices, passed_along(): return lax.ppermute(block, axis, route)  10.6 us
    convert_element_type x1, local copies, waits for them, and re-layouts, local(): jnp.einsum('goct,pit->gopci', row_kernel.astype(jnp.float32), one_hot)  7.73 us
    dot_general x1, matrix products, local(): jnp.einsum('goct,pit->gopci', row_kernel.astype(jnp.float32), one_hot)  5.63 us
  transfers between devices with their start and end apart: 4, of which 2 were waited for; matrix products, arithmetic and copies ran while one was open for 23% of the time, Pallas kernels for 0%

commit v1 on v0

v1 whole, which is shorter than its diff:
```python
import jax
import jax.numpy as jnp
from jax import lax
from jax.experimental import pallas as pl
from jax.experimental.pallas import tpu as pltpu
from jax.sharding import PartitionSpec as P

FAR, RING_TWIN, OWN, TWIN, RING = range(5)
FAR_CHUNKS = (3, 2, 2, 1)


def banded_kernel(odd_ref, rows_ref, out_ref):
    roles, lanes = out_ref.shape[1:3]
    width = rows_ref.shape[2]
    rows = lanes // width
    shape = (rows, lanes)
    row = lax.broadcasted_iota(jnp.int32, shape, 0)
    column = lax.rem(lax.broadcasted_iota(jnp.int32, shape, 1), rows)
    keep = column >= row
    odd = odd_ref[0]
    for role in range(roles):
        place = jnp.where(odd == 1, roles - 1 - role, role)
        for o in range(width):
            now = jnp.broadcast_to(rows_ref[0, place + 1, o : o + 1, :], shape)
            before = jnp.broadcast_to(rows_ref[0, place, o : o + 1, :], shape)
            now = pltpu.roll(now, 0, 1, stride=1, stride_axis=0)
            before = pltpu.roll(before, lanes - rows, 1, stride=1, stride_axis=0)
            out_ref[0, role, o * rows : (o + 1) * rows, :] = jnp.where(keep, now, before).astype(
                jnp.bfloat16
            )


def banded_matrices(row_kernel, odd, strip_rows):
    groups, width, _, taps = row_kernel.shape
    places = (taps - 1) // strip_rows + 1
    padded = jnp.pad(
        row_kernel.astype(jnp.float32),
        ((0, 0), (0, 0), (0, 0), (strip_rows, places * strip_rows - taps)),
    )
    lanes = width * strip_rows
    rows = padded.reshape(groups, width, width, places + 1, strip_rows)
    rows = jnp.transpose(rows, (0, 3, 1, 2, 4)).reshape(groups, places + 1, width, lanes)
    return pl.pallas_call(
        banded_kernel,
        grid=(groups,),
        in_specs=[
            pl.BlockSpec(memory_space=pltpu.SMEM),
            pl.BlockSpec((1, places + 1, width, lanes), lambda g: (g, 0, 0, 0)),
        ],
        out_specs=pl.BlockSpec((1, places, lanes, lanes), lambda g: (g, 0, 0, 0)),
        out_shape=jax.ShapeDtypeStruct((groups, places, lanes, lanes), jnp.bfloat16),
        cost_estimate=pl.CostEstimate(flops=10**9, bytes_accessed=4 * 10**6, transcendentals=0),
        name="banded",
    )(odd, rows)


def mix_kernel(bias_ref, weight_ref, x_ref, out_ref, wide_ref):
    channels, part, columns = x_ref.shape
    size = channels * part

    @pl.when((pl.program_id(0) == 0) & (pl.program_id(1) == 0))
    def _():
        spread = lax.broadcasted_iota(jnp.int32, (size, channels), 0) // part
        spread = (spread == lax.broadcasted_iota(jnp.int32, (size, channels), 1)).astype(jnp.float32)
        spread = spread.astype(jnp.bfloat16)
        weight = weight_ref[...]
        tall = lax.dot_general(
            spread, weight, (((1,), (1,)), ((), ())), preferred_element_type=jnp.float32
        ).astype(jnp.bfloat16)
        wide = lax.dot_general(
            tall, spread, (((1,), (1,)), ((), ())), preferred_element_type=jnp.float32
        )
        row = lax.broadcasted_iota(jnp.int32, (size, size), 0) % part
        column = lax.broadcasted_iota(jnp.int32, (size, size), 1) % part
        wide_ref[...] = jnp.where(row == column, wide, 0.0).astype(jnp.bfloat16)

    x = x_ref[...].astype(jnp.float32).reshape(size, columns).astype(jnp.bfloat16)
    total = jnp.dot(wide_ref[...], x, preferred_element_type=jnp.float32)
    for c in range(channels):
        out_ref[c] = total[c * part : (c + 1) * part] + bias_ref[c]


def mix(features, mix_weight, channel_bias):
    channels, rows, columns = features.shape
    part = 8
    half = columns // 2
    block = pl.BlockSpec((channels, part, half), lambda t, h: (0, t, h))
    return pl.pallas_call(
        mix_kernel,
        grid=(rows // part, 2),
        in_specs=[
            pl.BlockSpec(memory_space=pltpu.SMEM),
            pl.BlockSpec((channels, channels), lambda t, h: (0, 0)),
            block,
        ],
        out_specs=block,
        out_shape=jax.ShapeDtypeStruct(features.shape, jnp.float32),
        scratch_shapes=[pltpu.VMEM((channels * part, channels * part), jnp.bfloat16)],
        cost_estimate=pl.CostEstimate(
            flops=2 * part * channels * features.size,
            bytes_accessed=6 * features.size,
            transcendentals=0,
        ),
        name="mix",
    )(channel_bias, mix_weight, features)


def pair_kernel(first_matrix_ref, second_matrix_ref, first_ref, second_ref, part_ref, out_ref):
    width, rows, columns = first_ref.shape
    flat = (width * rows, columns)
    total = jnp.dot(
        first_matrix_ref[0, 0], first_ref[...].reshape(flat), preferred_element_type=jnp.float32
    )
    total += jnp.dot(
        second_matrix_ref[0, 0], second_ref[...].reshape(flat), preferred_element_type=jnp.float32
    )
    out_ref[...] = part_ref[...] + total.reshape(width, rows, columns)


def add_pair(matrices, first, first_role, second, second_role, part):
    groups, _, lanes, _ = matrices.shape
    channels, rows, columns = first.shape
    width = channels // groups
    strip = pl.BlockSpec((width, rows, columns), lambda g: (g, 0, 0))
    return pl.pallas_call(
        pair_kernel,
        grid=(groups,),
        in_specs=[
            pl.BlockSpec((1, 1, lanes, lanes), lambda g: (g, first_role, 0, 0)),
            pl.BlockSpec((1, 1, lanes, lanes), lambda g: (g, second_role, 0, 0)),
            strip,
            strip,
            strip,
        ],
        out_specs=strip,
        out_shape=jax.ShapeDtypeStruct(part.shape, jnp.float32),
        input_output_aliases={4: 0},
        cost_estimate=pl.CostEstimate(
            flops=4 * lanes * first.size, bytes_accessed=12 * first.size, transcendentals=0
        ),
    )(matrices, matrices, first, second, part)


def last_kernel(matrix_ref, far_ref, part_ref, *refs):
    out_ref = refs[-1]
    width, rows, columns = far_ref.shape
    total = jnp.dot(
        matrix_ref[0, 0],
        far_ref[...].reshape(width * rows, columns),
        preferred_element_type=jnp.float32,
    )
    total = part_ref[...] + total.reshape(width, rows, columns)
    out_ref[...] = jax.nn.gelu(total).astype(jnp.bfloat16)


def finish(matrices, far, part, out, start, count):
    groups, _, lanes, _ = matrices.shape
    channels, rows, columns = part.shape
    width = channels // groups
    here = pl.BlockSpec((width, rows, columns), lambda g: (g + start, 0, 0))
    given = [] if out is None else [out]
    return pl.pallas_call(
        last_kernel,
        grid=(count,),
        in_specs=[
            pl.BlockSpec((1, 1, lanes, lanes), lambda g: (g + start, FAR, 0, 0)),
            pl.BlockSpec((width, rows, columns), lambda g: (g, 0, 0)),
            here,
        ]
        + [pl.BlockSpec(memory_space=pl.ANY)] * len(given),
        out_specs=here,
        out_shape=jax.ShapeDtypeStruct(part.shape, jnp.bfloat16),
        input_output_aliases={3: 0} if given else {},
        cost_estimate=pl.CostEstimate(
            flops=2 * lanes * far.size, bytes_accessed=8 * far.size, transcendentals=far.size
        ),
    )(matrices, far, part, *given)


def local(features, row_kernel, mix_weight, channel_bias):
    _, strip_rows, _ = features.shape
    _, width = row_kernel.shape[:2]
    devices = lax.axis_size("strip")
    odd = lax.rem(lax.axis_index("strip"), 2).reshape(1)
    ring_route = [(i, (i + (2 if i % 2 else -2)) % devices) for i in range(devices)]
    far_route = [(i, (i + (1 if i % 2 else -1)) % devices) for i in range(devices)]
    twin_route = [(i, i ^ 1) for i in range(devices)]
    ring = lax.ppermute(features, "strip", ring_route)
    twin = lax.ppermute(features, "strip", twin_route)
    fars = []
    start = 0
    for count in FAR_CHUNKS:
        piece = twin[start * width : (start + count) * width]
        fars.append(lax.ppermute(piece, "strip", far_route))
        start += count
    ring_twin = lax.ppermute(ring, "strip", twin_route)
    matrices = banded_matrices(row_kernel, odd, strip_rows)
    part = mix(features, mix_weight, channel_bias)
    part = add_pair(matrices, features, OWN, twin, TWIN, part)
    part = add_pair(matrices, ring, RING, ring_twin, RING_TWIN, part)
    out = None
    start = 0
    for far, count in zip(fars, FAR_CHUNKS):
        out = finish(matrices, far, part, out, start, count)
        start += count
    return out


def solution(mesh):
    return jax.shard_map(
        local,
        mesh=mesh,
        in_specs=(P(None, "strip", None), P(), P(), P()),
        out_specs=P(None, "strip", None),
        check_vma=False,
    )
```

time: 196 us -> 138 us (0.70)
  Pallas kernels: 0 us -> 55.7 us
  waiting for transfers between devices: 101 us -> 46.4 us
  local copies, waits for them, and re-layouts: 49.3 us -> 9.36 us
  matrix products: 34.5 us -> 0 us
  starting transfers between devices: 10.6 us -> 25.1 us
    pallas_call x0 -> x8, Pallas kernels: none -> 55.7 us  [the longest x2 25.1 us: add_pair(): pl.pallas_call(pair_kernel, grid=(groups,), in_specs=[pl.BlockSpec((1, 1,...]
    ppermute x4 -> x7, waiting for transfers between devices: 101 us -> 46.4 us  [the longest x1 46.3 us: local(): ring = lax.ppermute(features, 'strip', ring_route)]
    dot_general x3 -> x0, matrix products: 34.5 us -> none  [the longest x1 15 us: local(): jnp.einsum('gab,gbw->gaw', matrix, data, preferred_element_type=jnp.float32)]
    unnamed x18 -> x6, local copies, waits for them, and re-layouts: 17.9 us -> 0.82 us
    ppermute x4 -> x7, starting transfers between devices: 10.6 us -> 25.1 us  [the longest x4 16.3 us: local(): fars.append(lax.ppermute(piece, 'strip', far_route))]
    convert_element_type x2 -> x0, local copies, waits for them, and re-layouts: 12.1 us -> none  [the longest x1 7.73 us: local(): jnp.einsum('goct,pit->gopci', row_kernel.astype(jnp.float32), one_hot)]
    reshape x1 -> x3, local copies, waits for them, and re-layouts: 14.2 us -> 4.44 us  [banded_matrices(): jnp.transpose(rows, (0, 3, 1, 2, 4))]
    concatenate x1 -> x0, local copies, waits for them, and re-layouts: 5.15 us -> none  [local(): joined = jnp.concatenate([above, features, below], axis=1)]
  transfers between devices with their start and end apart: 4 -> 7, of which waited for: 2 -> 1; matrix products, arithmetic and copies ran while one was open for 23% -> 6% of each run, Pallas kernels for 0% -> 39%
where the time goes in v1:
time: 138 us; the launch traced here: 137 us
  Pallas kernels  55.7 us (40%)
  waiting for transfers between devices  46.4 us (34%)
  starting transfers between devices  25.1 us (18%)
  local copies, waits for them, and re-layouts  9.36 us (7%)
    ppermute x1, waiting for transfers between devices, local(): ring = lax.ppermute(features, 'strip', ring_route)  46.3 us
    pallas_call x2, Pallas kernels, add_pair(): pl.pallas_call(pair_kernel, grid=(groups,), in_specs=[pl.BlockSpec((1, 1,...  25.1 us
    ppermute x4, starting transfers between devices, local(): fars.append(lax.ppermute(piece, 'strip', far_route))  16.3 us
    pallas_call x4, Pallas kernels, finish(): pl.pallas_call(last_kernel, grid=(count,), in_specs=[pl.BlockSpec((1, 1,...  14.5 us
    pallas_call x1, Pallas kernels, mix(): pl.pallas_call(mix_kernel, grid=(rows // part, 2), in_specs=[pl.BlockSpec...  9.25 us
    ppermute x1, starting transfers between devices, local(): ring = lax.ppermute(features, 'strip', ring_route)  8.79 us
    pallas_call x1, Pallas kernels, banded_matrices(): pl.pallas_call(banded_kernel, grid=(groups,), in_specs=[pl.BlockSpec(memo...  6.78 us
    reshape x3, local copies, waits for them, and re-layouts, banded_matrices(): jnp.transpose(rows, (0, 3, 1, 2, 4))  4.44 us
  transfers between devices with their start and end apart: 7, of which 1 were waited for; matrix products, arithmetic and copies ran while one was open for 6% of the time, Pallas kernels for 39%

profile of v1, /device:TPU:0, one launch (start us, length us, event | category | flops | bytes accessed | tf_op | source)
XLA Modules:
  0.0 136.7 jit_solution(17915410770449893291)
XLA Ops:
  0.0 8.8 %collective-permute-start.2 = (bf16[64,32,1024]{2,1,0:T(8,128)(2,1)}, bf16[64,32,1024]{2,1,0:T(8,128)(2,1)}, u32[]{:S(2)}, u32[]{:S(2)}) collective-permute-start(bf16[64,32,1024]{2,1,0:T(8,128)(2,1)} %first_ref.1), channel_id=1, source_target_pairs={{0,254},{1,3},{2,0},{3,5},{4,2},{5,7},{6,4},{7,9},{8,6},{9,11},{10... | collective-permute-start | bytes 12582920 | tf_op jit(solution)/shard_map/ppermute | solution.py:188
  8.8 0.0 collective-permute-start
  8.8 46.3 %collective-permute-done.2.first_ref = bf16[64,32,1024]{2,1,0:T(8,128)(2,1)} collective-permute-done((bf16[64,32,1024]{2,1,0:T(8,128)(2,1)}, bf16[64,32,1024]{2,1,0:T(8,128)(2,1)}, u32[]{:S(2)}, u32[]{:S(2)}) %collective-permute-start.2) | collective-permute-done | bytes 4194336 | tf_op jit(solution)/shard_map/ppermute | solution.py:188
  55.1 0.0 collective-permute-start.3
  55.1 1.5 %slice.19 = bf16[24,32,1024]{2,1,0:T(8,128)(2,1)} slice(bf16[64,32,1024]{2,1,0:T(8,128)(2,1)S(1)} %collective-permute-done.second_ref), slice={[0:24], [0:32], [0:1024]} | slice | bytes 3145728 | tf_op jit(solution)/shard_map/slice | solution.py:193
  56.6 8.0 %collective-permute-start.6 = (bf16[24,32,1024]{2,1,0:T(8,128)(2,1)}, bf16[24,32,1024]{2,1,0:T(8,128)(2,1)}, u32[]{:S(2)}, u32[]{:S(2)}) collective-permute-start(bf16[24,32,1024]{2,1,0:T(8,128)(2,1)} %slice.19), channel_id=1, source_target_pairs={{0,255},{1,2},{2,1},{3,4},{4,3},{5,6},{6,5},{7,8},{8,7},{9,10},{10... | collective-permute-start | bytes 4718600 | tf_op jit(solution)/shard_map/ppermute | solution.py:194
  64.6 1.6 %fusion = (bf16[16,32,1024]{2,1,0:T(8,128)(2,1)}, bf16[16,32,1024]{2,1,0:T(8,128)(2,1)}) fusion(bf16[64,32,1024]{2,1,0:T(8,128)(2,1)S(1)} %collective-permute-done.second_ref), kind=kLoop, calls=%fused_computation.1 | loop fusion | bytes 4194304 | tf_op jit(solution)/shard_map/slice | solution.py:193
  66.2 1.0 collective-permute-start.5
  67.2 6.2 %collective-permute-start.4 = (bf16[16,32,1024]{2,1,0:T(8,128)(2,1)}, bf16[16,32,1024]{2,1,0:T(8,128)(2,1)}, u32[]{:S(2)}, u32[]{:S(2)}) collective-permute-start(bf16[16,32,1024]{2,1,0:T(8,128)(2,1)} %get-tuple-element.6), channel_id=1, source_target_pairs={{0,255},{1,2},{2,1},{3,4},{4,3},{5,6},{6,5},{7,8},{8,7},{9,10},{10... | collective-permute-start | bytes 3145736 | tf_op jit(solution)/shard_map/ppermute | solution.py:194
  73.4 0.1 pad_convert_fusion
  73.5 0.4 reshape.20
  73.9 1.4 %copy.11 = f32[8,6,8,8,32]{4,3,2,1,0:T(8,128)} copy(f32[8,6,8,8,32]{4,1,3,2,0:T(8,128)S(1)} %bitcast.6) | data formatting | bytes 786432 | tf_op jit(solution)/shard_map/reshape | solution.py:42
  75.3 2.6 %reshape.17.rows_ref = f32[8,6,8,256]{3,2,1,0:T(8,128)} reshape(f32[8,6,8,8,32]{4,3,2,1,0:T(8,128)} %copy.11) | data formatting | bytes 786432 | tf_op jit(solution)/shard_map/reshape | solution.py:42
  78.0 9.3 %mix.1.part_ref = f32[64,32,1024]{2,1,0:T(8,128)} custom-call(f32[64]{0:T(128)} %bias_ref.1, bf16[64,64]{1,0:T(8,128)(2,1)} %weight_ref.1, bf16[64,32,1024]{2,1,0:T(8,128)(2,1)} %first_ref.1), custom_call_target="tpu_custom_call" | custom-call | flops 2147483648 | bytes 12582912 | tf_op jit(solution)/shard_map/mix/pallas_call | solution.py:88
  87.2 1.1 slice.16
  88.3 1.1 collective-permute-start.1
  89.4 6.8 %banded.1.first_matrix_ref.second_matrix_ref.matrix_ref = bf16[8,5,256,256]{3,2,1,0:T(8,128)(2,1)} custom-call(s32[1]{0:T(128)} %bitcast.odd_ref, f32[8,6,8,256]{3,2,1,0:T(8,128)} %reshape.17.rows_ref), custom_call_target="tpu_custom_call" | custom-call | flops 1000000000 | bytes 4000000 | tf_op jit(solution)/shard_map/banded/pallas_call | solution.py:43
  96.2 12.6 %shard_map.46.part_ref = f32[64,32,1024]{2,1,0:T(8,128)} custom-call(bf16[8,5,256,256]{3,2,1,0:T(8,128)(2,1)} %banded.1.first_matrix_ref.second_matrix_ref.matrix_ref, bf16[8,5,256,256]{3,2,1,0:T(8,128)(2,1)} %banded.1.first_matrix_ref.second_matrix_ref.matrix_ref, bf16[64,32,1024]{2,1,0:T(8,128)(2,1)} %first_ref.1, ...), custom_call_target="tpu_custom_call", output_to_operand_aliasing={{}: (4, {})} | custom-call | flops 2147483648 | bytes 25165824 | tf_op jit(solution)/shard_map/pallas_call | solution.py:125
  108.7 12.6 %shard_map.47.part_ref = f32[64,32,1024]{2,1,0:T(8,128)} custom-call(bf16[8,5,256,256]{3,2,1,0:T(8,128)(2,1)} %banded.1.first_matrix_ref.second_matrix_ref.matrix_ref, bf16[8,5,256,256]{3,2,1,0:T(8,128)(2,1)} %banded.1.first_matrix_ref.second_matrix_ref.matrix_ref, ...), custom_call_target="tpu_custom_call", output_to_operand_aliasing={{}: (4, {})} | custom-call | flops 2147483648 | bytes 25165824 | tf_op jit(solution)/shard_map/pallas_call | solution.py:125
  121.3 5.1 %shard_map.48.refs_0_ = bf16[64,32,1024]{2,1,0:T(8,128)(2,1)} custom-call(bf16[8,5,256,256]{3,2,1,0:T(8,128)(2,1)} %banded.1.first_matrix_ref.second_matrix_ref.matrix_ref, bf16[24,32,1024]{2,1,0:T(8,128)(2,1)} %collective-permute-done.6.far_ref, f32[64,32,1024]{2,1,0:T(8,128)} %shard_map.47.part_ref), custom_call_target="tpu_custom_call" | custom-call | flops 402653184 | bytes 6291456 | tf_op jit(solution)/shard_map/pallas_call | solution.py:162
  126.4 3.3 %shard_map.49.refs_0_ = bf16[64,32,1024]{2,1,0:T(8,128)(2,1)} custom-call(bf16[8,5,256,256]{3,2,1,0:T(8,128)(2,1)} %banded.1.first_matrix_ref.second_matrix_ref.matrix_ref, bf16[16,32,1024]{2,1,0:T(8,128)(2,1)} %collective-permute-done.5.far_ref, f32[64,32,1024]{2,1,0:T(8,128)} %shard_map.47.part_ref, ...), custom_call_target="tpu_custom_call", output_to_operand_aliasing={{}: (3, {})} | custom-call | flops 268435456 | bytes 4194304 | tf_op jit(solution)/shard_map/pallas_call | solution.py:162
  129.8 3.3 %shard_map.50.refs_0_ = bf16[64,32,1024]{2,1,0:T(8,128)(2,1)} custom-call(bf16[8,5,256,256]{3,2,1,0:T(8,128)(2,1)} %banded.1.first_matrix_ref.second_matrix_ref.matrix_ref, bf16[16,32,1024]{2,1,0:T(8,128)(2,1)} %collective-permute-done.4.far_ref, f32[64,32,1024]{2,1,0:T(8,128)} %shard_map.47.part_ref, ...), custom_call_target="tpu_custom_call", output_to_operand_aliasing={{}: (3, {})} | custom-call | flops 268435456 | bytes 4194304 | tf_op jit(solution)/shard_map/pallas_call | solution.py:162
  133.1 0.8 copy-done.1
  133.9 2.8 %shard_map.51 = bf16[64,32,1024]{2,1,0:T(8,128)(2,1)} custom-call(bf16[8,5,256,256]{3,2,1,0:T(8,128)(2,1)} %banded.1.first_matrix_ref.second_matrix_ref.matrix_ref, bf16[8,32,1024]{2,1,0:T(8,128)(2,1)} %copy-done.1, f32[64,32,1024]{2,1,0:T(8,128)} %shard_map.47.part_ref, bf16[64,32,1024]{2,1,0:T(8,128)(2,1)} %shard_map.50.refs_0_), custom_call_target="tpu_custom_call", output_to_operand_aliasing={{}: (3, {})} | custom-call | flops 134217728 | bytes 2097152 | tf_op jit(solution)/shard_map/pallas_call | solution.py:162
  (11 shorter events, 0.0 us)
Async XLA Ops:
  0.0 73.4 %copy-start.2 = (bf16[8,8,8,129]{3,2,1,0:T(8,128)(2,1)S(1)}, bf16[8,8,8,129]{3,2,1,0:T(8,128)(2,1)}, u32[]{:S(2)}) copy-start(bf16[8,8,8,129]{3,2,1,0:T(8,128)(2,1)} %param.5) | copy-start | bytes 396292
  0.0 55.1 %collective-permute-start.2 = (bf16[64,32,1024]{2,1,0:T(8,128)(2,1)}, bf16[64,32,1024]{2,1,0:T(8,128)(2,1)}, u32[]{:S(2)}, u32[]{:S(2)}) collective-permute-start(bf16[64,32,1024]{2,1,0:T(8,128)(2,1)} %first_ref.1), channel_id=1, source_target_pairs={{0,254},{1,3},{2,0},{3,5},{4,2},{5,7},{6,4},{7,9},{8,6},{9,11},{10... | collective-permute-start | bytes 12582920 | tf_op jit(solution)/shard_map/ppermute | solution.py:188
  8.8 46.3 %collective-permute-start = (bf16[64,32,1024]{2,1,0:T(8,128)(2,1)}, bf16[64,32,1024]{2,1,0:T(8,128)(2,1)S(1)}, u32[]{:S(2)}, u32[]{:S(2)}) collective-permute-start(bf16[64,32,1024]{2,1,0:T(8,128)(2,1)} %first_ref.1), channel_id=1, source_target_pairs={{0,1},{1,0},{2,3},{3,2},{4,5},{5,4},{6,7},{7,6},{8,9},{9,8},{10,11... | collective-permute-start | bytes 12582920 | tf_op jit(solution)/shard_map/ppermute | solution.py:189
  55.1 53.6 %collective-permute-start.3 = (bf16[64,32,1024]{2,1,0:T(8,128)(2,1)}, bf16[64,32,1024]{2,1,0:T(8,128)(2,1)}, u32[]{:S(2)}, u32[]{:S(2)}) collective-permute-start(bf16[64,32,1024]{2,1,0:T(8,128)(2,1)} %collective-permute-done.2.first_ref), channel_id=1, source_target_pairs={{0,1},{1,0},{2,3},{3,2},{4,5},{5,4},{6,7},{7,6},{8,9},{9,8},{10,11... | collective-permute-start | bytes 12582920 | tf_op jit(solution)/shard_map/ppermute | solution.py:196
  55.1 9.5 %copy-start = (bf16[64,32,1024]{2,1,0:T(8,128)(2,1)}, bf16[64,32,1024]{2,1,0:T(8,128)(2,1)S(1)}, u32[]{:S(2)}) copy-start(bf16[64,32,1024]{2,1,0:T(8,128)(2,1)S(1)} %collective-permute-done.second_ref) | copy-start | bytes 12582916
  56.6 64.7 %collective-permute-start.6 = (bf16[24,32,1024]{2,1,0:T(8,128)(2,1)}, bf16[24,32,1024]{2,1,0:T(8,128)(2,1)}, u32[]{:S(2)}, u32[]{:S(2)}) collective-permute-start(bf16[24,32,1024]{2,1,0:T(8,128)(2,1)} %slice.19), channel_id=1, source_target_pairs={{0,255},{1,2},{2,1},{3,4},{4,3},{5,6},{6,5},{7,8},{8,7},{9,10},{10... | collective-permute-start | bytes 4718600 | tf_op jit(solution)/shard_map/ppermute | solution.py:194
  66.2 60.2 %collective-permute-start.5 = (bf16[16,32,1024]{2,1,0:T(8,128)(2,1)}, bf16[16,32,1024]{2,1,0:T(8,128)(2,1)}, u32[]{:S(2)}, u32[]{:S(2)}) collective-permute-start(bf16[16,32,1024]{2,1,0:T(8,128)(2,1)} %get-tuple-element.5), channel_id=1, source_target_pairs={{0,255},{1,2},{2,1},{3,4},{4,3},{5,6},{6,5},{7,8},{8,7},{9,10},{10... | collective-permute-start | bytes 3145736 | tf_op jit(solution)/shard_map/ppermute | solution.py:194
  67.2 62.6 %collective-permute-start.4 = (bf16[16,32,1024]{2,1,0:T(8,128)(2,1)}, bf16[16,32,1024]{2,1,0:T(8,128)(2,1)}, u32[]{:S(2)}, u32[]{:S(2)}) collective-permute-start(bf16[16,32,1024]{2,1,0:T(8,128)(2,1)} %get-tuple-element.6), channel_id=1, source_target_pairs={{0,255},{1,2},{2,1},{3,4},{4,3},{5,6},{6,5},{7,8},{8,7},{9,10},{10... | collective-permute-start | bytes 3145736 | tf_op jit(solution)/shard_map/ppermute | solution.py:194
  88.3 44.8 %collective-permute-start.1 = (bf16[8,32,1024]{2,1,0:T(8,128)(2,1)S(1)}, bf16[8,32,1024]{2,1,0:T(8,128)(2,1)S(1)}, u32[]{:S(2)}, u32[]{:S(2)}) collective-permute-start(bf16[8,32,1024]{2,1,0:T(8,128)(2,1)S(1)} %slice.16), channel_id=1, source_target_pairs={{0,255},{1,2},{2,1},{3,4},{4,3},{5,6},{6,5},{7,8},{8,7},{9,10},{10... | collective-permute-start | bytes 1572872 | tf_op jit(solution)/shard_map/ppermute | solution.py:194
  133.1 0.8 copy-start.1

commit v2 on v1

--- a/solution.py
+++ b/solution.py
@@ -1,3 +1,5 @@
+import functools
+
 import jax
 import jax.numpy as jnp
 from jax import lax
@@ -6,10 +8,13 @@
 from jax.sharding import PartitionSpec as P
 
 FAR, RING_TWIN, OWN, TWIN, RING = range(5)
-FAR_CHUNKS = (3, 2, 2, 1)
+FAR_CHUNKS = (4, 3, 1)
+WHOLE = pl.BlockSpec(memory_space=pltpu.VMEM)
+GRANT = pltpu.CompilerParams(vmem_limit_bytes=16 * 2**20)
 
 
 def banded_kernel(odd_ref, rows_ref, out_ref):
+    g = pl.program_id(0)
     roles, lanes = out_ref.shape[1:3]
     width = rows_ref.shape[2]
     rows = lanes // width
@@ -25,7 +30,7 @@
             before = jnp.broadcast_to(rows_ref[0, place, o : o + 1, :], shape)
             now = pltpu.roll(now, 0, 1, stride=1, stride_axis=0)
             before = pltpu.roll(before, lanes - rows, 1, stride=1, stride_axis=0)
-            out_ref[0, role, o * rows : (o + 1) * rows, :] = jnp.where(keep, now, before).astype(
+            out_ref[g, role, o * rows : (o + 1) * rows, :] = jnp.where(keep, now, before).astype(
                 jnp.bfloat16
             )
 
@@ -47,8 +52,9 @@
             pl.BlockSpec(memory_space=pltpu.SMEM),
             pl.BlockSpec((1, places + 1, width, lanes), lambda g: (g, 0, 0, 0)),
         ],
-        out_specs=pl.BlockSpec((1, places, lanes, lanes), lambda g: (g, 0, 0, 0)),
-        out_shape=jax.ShapeDtypeStruct((groups, places, lanes, lanes), jnp.bfloat16),
+        out_specs=WHOLE,
+        out_shape=pltpu.VMEM((groups, places, lanes, lanes), jnp.bfloat16),
+        compiler_params=GRANT,
         cost_estimate=pl.CostEstimate(flops=10**9, bytes_accessed=4 * 10**6, transcendentals=0),
         name="banded",
     )(odd, rows)
@@ -76,8 +82,10 @@
 
     x = x_ref[...].astype(jnp.float32).reshape(size, columns).astype(jnp.bfloat16)
     total = jnp.dot(wide_ref[...], x, preferred_element_type=jnp.float32)
+    rows = pl.ds(pl.multiple_of(pl.program_id(0) * part, part), part)
+    lanes = pl.ds(pl.multiple_of(pl.program_id(1) * columns, columns), columns)
     for c in range(channels):
-        out_ref[c] = total[c * part : (c + 1) * part] + bias_ref[c]
+        out_ref[c, rows, lanes] = total[c * part : (c + 1) * part] + bias_ref[c]
 
 
 def mix(features, mix_weight, channel_bias):
@@ -93,8 +101,9 @@
             pl.BlockSpec((channels, channels), lambda t, h: (0, 0)),
             block,
         ],
-        out_specs=block,
-        out_shape=jax.ShapeDtypeStruct(features.shape, jnp.float32),
+        out_specs=WHOLE,
+        out_shape=pltpu.VMEM(features.shape, jnp.float32),
+        compiler_params=GRANT,
         scratch_shapes=[pltpu.VMEM((channels * part, channels * part), jnp.bfloat16)],
         cost_estimate=pl.CostEstimate(
             flops=2 * part * channels * features.size,
@@ -105,16 +114,18 @@
     )(channel_bias, mix_weight, features)
 
 
-def pair_kernel(first_matrix_ref, second_matrix_ref, first_ref, second_ref, part_ref, out_ref):
+def pair_kernel(first_role, second_role, matrix_ref, first_ref, second_ref, part_ref, out_ref):
+    g = pl.program_id(0)
     width, rows, columns = first_ref.shape
     flat = (width * rows, columns)
     total = jnp.dot(
-        first_matrix_ref[0, 0], first_ref[...].reshape(flat), preferred_element_type=jnp.float32
+        matrix_ref[g, first_role], first_ref[...].reshape(flat), preferred_element_type=jnp.float32
     )
     total += jnp.dot(
-        second_matrix_ref[0, 0], second_ref[...].reshape(flat), preferred_element_type=jnp.float32
-    )
-    out_ref[...] = part_ref[...] + total.reshape(width, rows, columns)
+        matrix_ref[g, second_role], second_ref[...].reshape(flat), preferred_element_type=jnp.float32
+    )
+    here = pl.ds(g * width, width)
+    out_ref[here] = part_ref[here] + total.reshape(width, rows, columns)
 
 
 def add_pair(matrices, first, first_role, second, second_role, part):
@@ -123,63 +134,83 @@
     width = channels // groups
     strip = pl.BlockSpec((width, rows, columns), lambda g: (g, 0, 0))
     return pl.pallas_call(
-        pair_kernel,
+        functools.partial(pair_kernel, first_role, second_role),
         grid=(groups,),
-        in_specs=[
-            pl.BlockSpec((1, 1, lanes, lanes), lambda g: (g, first_role, 0, 0)),
-            pl.BlockSpec((1, 1, lanes, lanes), lambda g: (g, second_role, 0, 0)),
-            strip,
-            strip,
-            strip,
-        ],
-        out_specs=strip,
-        out_shape=jax.ShapeDtypeStruct(part.shape, jnp.float32),
-        input_output_aliases={4: 0},
+        in_specs=[WHOLE, strip, strip, WHOLE],
+        out_specs=WHOLE,
+        out_shape=pltpu.VMEM(part.shape, jnp.float32),
+        input_output_aliases={3: 0},
+        compiler_params=GRANT,
         cost_estimate=pl.CostEstimate(
-            flops=4 * lanes * first.size, bytes_accessed=12 * first.size, transcendentals=0
+            flops=4 * lanes * first.size, bytes_accessed=4 * first.size, transcendentals=0
         ),
-    )(matrices, matrices, first, second, part)
-
-
-def last_kernel(matrix_ref, far_ref, part_ref, *refs):
-    out_ref = refs[-1]
-    width, rows, columns = far_ref.shape
-    total = jnp.dot(
-        matrix_ref[0, 0],
-        far_ref[...].reshape(width * rows, columns),
-        preferred_element_type=jnp.float32,
-    )
-    total = part_ref[...] + total.reshape(width, rows, columns)
-    out_ref[...] = jax.nn.gelu(total).astype(jnp.bfloat16)
-
-
-def finish(matrices, far, part, out, start, count):
+    )(matrices, first, second, part)
+
+
+def last_kernel(start, count, matrix_ref, part_ref, far_ref, *refs):
+    out_ref, ready_ref, sems = refs[-3:]
+    width = ready_ref.shape[0] // count
+    rows, columns = ready_ref.shape[1:]
+    tile = columns // 2
+
+    def copy(g, t):
+        lanes = pl.ds(t * tile, tile)
+        return pltpu.make_async_copy(
+            ready_ref.at[pl.ds(g * width, width), :, lanes],
+            out_ref.at[pl.ds((start + g) * width, width), :, lanes],
+            sems.at[2 * g + t],
+        )
+
+    def group(g):
+        here = pl.ds(g * width, width)
+        for t in range(2):
+            lanes = slice(t * tile, (t + 1) * tile)
+            total = jnp.dot(
+                matrix_ref[start + g, FAR],
+                far_ref[here, :, lanes].reshape(width * rows, tile),
+                preferred_element_type=jnp.float32,
+            )
+            total = part_ref[pl.ds((start + g) * width, width), :, lanes] + total.reshape(
+                width, rows, tile
+            )
+            ready_ref[here, :, lanes] = jax.nn.gelu(total).astype(jnp.bfloat16)
+            copy(g, t).start()
+
+    if count == 1:
+        group(0)
+    else:
+        pl.loop(0, count)(group)
+    for g in range(count):
+        for t in range(2):
+            copy(g, t).wait()
+
+
+def finish(matrices, part, far, out, start, count):
     groups, _, lanes, _ = matrices.shape
     channels, rows, columns = part.shape
     width = channels // groups
-    here = pl.BlockSpec((width, rows, columns), lambda g: (g + start, 0, 0))
     given = [] if out is None else [out]
-    return pl.pallas_call(
-        last_kernel,
-        grid=(count,),
-        in_specs=[
-            pl.BlockSpec((1, 1, lanes, lanes), lambda g: (g + start, FAR, 0, 0)),
-            pl.BlockSpec((width, rows, columns), lambda g: (g, 0, 0)),
-            here,
-        ]
-        + [pl.BlockSpec(memory_space=pl.ANY)] * len(given),
-        out_specs=here,
+    whole = pl.BlockSpec(memory_space=pl.ANY)
+    return pl.pallas_call(
+        functools.partial(last_kernel, start, count),
+        in_specs=[WHOLE] * 3 + [whole] * len(given),
+        out_specs=whole,
         out_shape=jax.ShapeDtypeStruct(part.shape, jnp.bfloat16),
         input_output_aliases={3: 0} if given else {},
+        scratch_shapes=[
+            pltpu.VMEM((count * width, rows, columns), jnp.bfloat16),
+            pltpu.SemaphoreType.DMA((2 * count,)),
+        ],
+        compiler_params=GRANT,
         cost_estimate=pl.CostEstimate(
-            flops=2 * lanes * far.size, bytes_accessed=8 * far.size, transcendentals=far.size
+            flops=2 * lanes * far.size, bytes_accessed=4 * far.size, transcendentals=far.size
         ),
-    )(matrices, far, part, *given)
+    )(matrices, part, far, *given)
 
 
 def local(features, row_kernel, mix_weight, channel_bias):
-    _, strip_rows, _ = features.shape
-    _, width = row_kernel.shape[:2]
+    strip_rows = features.shape[1]
+    width = row_kernel.shape[1]
     devices = lax.axis_size("strip")
     odd = lax.rem(lax.axis_index("strip"), 2).reshape(1)
     ring_route = [(i, (i + (2 if i % 2 else -2)) % devices) for i in range(devices)]
@@ -201,7 +232,7 @@
     out = None
     start = 0
     for far, count in zip(fars, FAR_CHUNKS):
-        out = finish(matrices, far, part, out, start, count)
+        out = finish(matrices, part, far, out, start, count)
         start += count
     return out
 

time: 138 us -> 113 us (0.82)
  Pallas kernels: 55.7 us -> 27.1 us
  waiting for transfers between devices: 46.4 us -> 49.2 us
  local copies, waits for them, and re-layouts: 9.36 us -> 11.8 us
    pallas_call x6 -> x5, Pallas kernels: 39.6 us -> 18.8 us  [the longest x2 10.9 us: add_pair(): pl.pallas_call(functools.partial(pair_kernel, first_role, second_role), g...]
    pallas_call x1, Pallas kernels: 9.25 us -> 4.94 us  [mix(): pl.pallas_call(mix_kernel, grid=(rows // part, 2), in_specs=[pl.BlockSpec...]
    pallas_call x1, Pallas kernels: 6.78 us -> 3.35 us  [banded_matrices(): pl.pallas_call(banded_kernel, grid=(groups,), in_specs=[pl.BlockSpec(memo...]
    ppermute x4 -> x3, waiting for transfers between devices: 0.01 us -> 2.91 us  [local(): fars.append(lax.ppermute(piece, 'strip', far_route))]
    reshape x3, local copies, waits for them, and re-layouts: 4.44 us -> 6.57 us  [banded_matrices(): jnp.transpose(rows, (0, 3, 1, 2, 4))]
    unnamed x6 -> x14, local copies, waits for them, and re-layouts: 0.82 us -> 2.21 us
    ppermute x4 -> x3, starting transfers between devices: 16.3 us -> 15.3 us  [local(): fars.append(lax.ppermute(piece, 'strip', far_route))]
  transfers between devices with their start and end apart: 7 -> 6, of which waited for: 1 -> 3; matrix products, arithmetic and copies ran while one was open for 6% -> 9% of each run, Pallas kernels for 39% -> 23%
where the time goes in v2:
time: 113 us; the launch traced here: 112 us
  waiting for transfers between devices  49.2 us (44%)
  Pallas kernels  27.1 us (24%)
  starting transfers between devices  24.1 us (21%)
  local copies, waits for them, and re-layouts  11.8 us (10%)
    ppermute x1, waiting for transfers between devices, local(): ring = lax.ppermute(features, 'strip', ring_route)  46.3 us
    ppermute x3, starting transfers between devices, local(): fars.append(lax.ppermute(piece, 'strip', far_route))  15.3 us
    pallas_call x2, Pallas kernels, add_pair(): pl.pallas_call(functools.partial(pair_kernel, first_role, second_role), g...  10.9 us
    ppermute x1, starting transfers between devices, local(): ring = lax.ppermute(features, 'strip', ring_route)  8.79 us
    pallas_call x3, Pallas kernels, finish(): pl.pallas_call(functools.partial(last_kernel, start, count), in_specs=[WH...  7.92 us
    reshape x3, local copies, waits for them, and re-layouts, banded_matrices(): jnp.transpose(rows, (0, 3, 1, 2, 4))  6.57 us
    pallas_call x1, Pallas kernels, mix(): pl.pallas_call(mix_kernel, grid=(rows // part, 2), in_specs=[pl.BlockSpec...  4.94 us
    pallas_call x1, Pallas kernels, banded_matrices(): pl.pallas_call(banded_kernel, grid=(groups,), in_specs=[pl.BlockSpec(memo...  3.35 us
  transfers between devices with their start and end apart: 6, of which 3 were waited for; matrix products, arithmetic and copies ran while one was open for 9% of the time, Pallas kernels for 23%

profile of v2, /device:TPU:0, one launch (start us, length us, event | category | flops | bytes accessed | tf_op | source)
XLA Modules:
  0.0 112.5 jit_solution(14717580912707778517)
XLA Ops:
  0.0 8.8 %collective-permute-start = (bf16[64,32,1024]{2,1,0:T(8,128)(2,1)}, bf16[64,32,1024]{2,1,0:T(8,128)(2,1)}, u32[]{:S(2)}, u32[]{:S(2)}) collective-permute-start(bf16[64,32,1024]{2,1,0:T(8,128)(2,1)} %first_ref.1), channel_id=1, source_target_pairs={{0,254},{1,3},{2,0},{3,5},{4,2},{5,7},{6,4},{7,9},{8,6},{9,11},{10... | collective-permute-start | bytes 12582920 | tf_op jit(solution)/shard_map/ppermute | solution.py:219
  8.8 46.3 %collective-permute-done.first_ref = bf16[64,32,1024]{2,1,0:T(8,128)(2,1)} collective-permute-done((bf16[64,32,1024]{2,1,0:T(8,128)(2,1)}, bf16[64,32,1024]{2,1,0:T(8,128)(2,1)}, u32[]{:S(2)}, u32[]{:S(2)}) %collective-permute-start) | collective-permute-done | bytes 4194336 | tf_op jit(solution)/shard_map/ppermute | solution.py:219
  55.1 1.7 %slice.14 = bf16[32,32,1024]{2,1,0:T(8,128)(2,1)} slice(bf16[64,32,1024]{2,1,0:T(8,128)(2,1)S(1)} %collective-permute-done.2.second_ref), slice={[0:32], [0:32], [0:1024]} | slice | bytes 4194304 | tf_op jit(solution)/shard_map/slice | solution.py:224
  56.8 8.0 %collective-permute-start.5 = (bf16[32,32,1024]{2,1,0:T(8,128)(2,1)}, bf16[32,32,1024]{2,1,0:T(8,128)(2,1)S(1)}, u32[]{:S(2)}, u32[]{:S(2)}) collective-permute-start(bf16[32,32,1024]{2,1,0:T(8,128)(2,1)} %slice.14), channel_id=1, source_target_pairs={{0,255},{1,2},{2,1},{3,4},{4,3},{5,6},{6,5},{7,8},{8,7},{9,10},{10... | collective-permute-start | bytes 6291464 | tf_op jit(solution)/shard_map/ppermute | solution.py:225
  64.8 1.3 %slice.13 = bf16[24,32,1024]{2,1,0:T(8,128)(2,1)} slice(bf16[64,32,1024]{2,1,0:T(8,128)(2,1)S(1)} %collective-permute-done.2.second_ref), slice={[32:56], [0:32], [0:1024]} | slice | bytes 3145728 | tf_op jit(solution)/shard_map/slice | solution.py:224
  66.1 1.0 collective-permute-start.4
  67.1 0.1 pad_convert_fusion
  67.3 0.0 copy-start.5
  67.3 1.7 %reshape.20 = f32[8,8,8,6,32]{4,3,2,1,0:T(8,128)} reshape(f32[8,8,8,192]{3,2,1,0:T(8,128)S(1)} %pad_convert_fusion) | data formatting | bytes 786432 | tf_op jit(solution)/shard_map/reshape | solution.py:47
  69.0 3.0 %copy.10 = f32[8,6,8,8,32]{4,3,2,1,0:T(8,128)} copy(f32[8,6,8,8,32]{4,1,3,2,0:T(8,128)} %bitcast.6) | data formatting | bytes 786432 | tf_op jit(solution)/shard_map/reshape | solution.py:47
  72.0 1.9 %reshape.17.rows_ref = f32[8,6,8,256]{3,2,1,0:T(8,128)S(1)} reshape(f32[8,6,8,8,32]{4,3,2,1,0:T(8,128)} %copy.10) | data formatting | bytes 786432 | tf_op jit(solution)/shard_map/reshape | solution.py:47
  73.9 0.0 copy-start
  73.9 2.2 %copy-done = bf16[64,32,1024]{2,1,0:T(8,128)(2,1)S(1)} copy-done((bf16[64,32,1024]{2,1,0:T(8,128)(2,1)S(1)}, bf16[64,32,1024]{2,1,0:T(8,128)(2,1)}, u32[]{:S(2)}) %copy-start) | copy-done | bytes 4194328
  76.1 4.9 %mix.1.part_ref = f32[64,32,1024]{2,1,0:T(8,128)S(1)} custom-call(f32[64]{0:T(128)S(1)} %copy-done.5, bf16[64,64]{1,0:T(8,128)(2,1)S(1)} %copy-done.4, bf16[64,32,1024]{2,1,0:T(8,128)(2,1)S(1)} %copy-done), custom_call_target="tpu_custom_call" | custom-call | flops 2147483648 | bytes 12582912 | tf_op jit(solution)/shard_map/mix/pallas_call | solution.py:96
  81.0 0.0 copy-start.1
  81.1 6.3 %collective-permute-start.3 = (bf16[8,32,1024]{2,1,0:T(8,128)(2,1)S(1)}, bf16[8,32,1024]{2,1,0:T(8,128)(2,1)S(1)}, u32[]{:S(2)}, u32[]{:S(2)}) collective-permute-start(bf16[8,32,1024]{2,1,0:T(8,128)(2,1)S(1)} %slice.12), channel_id=1, source_target_pairs={{0,255},{1,2},{2,1},{3,4},{4,3},{5,6},{6,5},{7,8},{8,7},{9,10},{10... | collective-permute-start | bytes 1572872 | tf_op jit(solution)/shard_map/ppermute | solution.py:225
  87.4 3.3 %banded.1.matrix_ref = bf16[8,5,256,256]{3,2,1,0:T(8,128)(2,1)S(1)} custom-call(s32[1]{0:T(128)} %bitcast.odd_ref, f32[8,6,8,256]{3,2,1,0:T(8,128)S(1)} %reshape.17.rows_ref), custom_call_target="tpu_custom_call" | custom-call | flops 1000000000 | bytes 4000000 | tf_op jit(solution)/shard_map/banded/pallas_call | solution.py:48
  90.7 3.6 %shard_map.46.part_ref = f32[64,32,1024]{2,1,0:T(8,128)S(1)} custom-call(bf16[8,5,256,256]{3,2,1,0:T(8,128)(2,1)S(1)} %banded.1.matrix_ref, bf16[64,32,1024]{2,1,0:T(8,128)(2,1)S(1)} %copy-done.1, bf16[64,32,1024]{2,1,0:T(8,128)(2,1)S(1)} %copy-done.3, f32[64,32,1024]{2,1,0:T(8,128)S(1)} %mix.1.part_ref), custom_call_target="tpu_custom_call", output_to_operand_aliasing={{}: (3, {})} | custom-call | flops 2147483648 | bytes 8388608 | tf_op jit(solution)/shard_map/pallas_call | solution.py:136
  94.4 7.3 %shard_map.47.part_ref = f32[64,32,1024]{2,1,0:T(8,128)S(1)} custom-call(bf16[8,5,256,256]{3,2,1,0:T(8,128)(2,1)S(1)} %banded.1.matrix_ref, bf16[64,32,1024]{2,1,0:T(8,128)(2,1)} %collective-permute-done.first_ref, bf16[64,32,1024]{2,1,0:T(8,128)(2,1)} %collective-permute-done.1.second_ref, ...), custom_call_target="tpu_custom_call", output_to_operand_aliasing={{}: (3, {})} | custom-call | flops 2147483648 | bytes 8388608 | tf_op jit(solution)/shard_map/pallas_call | solution.py:136
  101.7 2.9 %shard_map.48.refs_0_ = bf16[64,32,1024]{2,1,0:T(8,128)(2,1)} custom-call(bf16[8,5,256,256]{3,2,1,0:T(8,128)(2,1)S(1)} %banded.1.matrix_ref, f32[64,32,1024]{2,1,0:T(8,128)S(1)} %shard_map.47.part_ref, bf16[32,32,1024]{2,1,0:T(8,128)(2,1)S(1)} %collective-permute-done.5.far_ref), custom_call_target="tpu_custom_call" | custom-call | flops 536870912 | bytes 4194304 | tf_op jit(solution)/shard_map/pallas_call | solution.py:194
  104.6 1.2 %collective-permute-done.4.far_ref = bf16[24,32,1024]{2,1,0:T(8,128)(2,1)} collective-permute-done((bf16[24,32,1024]{2,1,0:T(8,128)(2,1)}, bf16[24,32,1024]{2,1,0:T(8,128)(2,1)}, u32[]{:S(2)}, u32[]{:S(2)}) %collective-permute-start.4) | collective-permute-done | bytes 1572896 | tf_op jit(solution)/shard_map/ppermute | solution.py:225
  105.7 3.8 %shard_map.49.refs_0_ = bf16[64,32,1024]{2,1,0:T(8,128)(2,1)} custom-call(bf16[8,5,256,256]{3,2,1,0:T(8,128)(2,1)S(1)} %banded.1.matrix_ref, f32[64,32,1024]{2,1,0:T(8,128)S(1)} %shard_map.47.part_ref, bf16[24,32,1024]{2,1,0:T(8,128)(2,1)} %collective-permute-done.4.far_ref, bf16[64,32,1024]{2,1,0:T(8,128)(2,1)} %shard_map.48.refs_0_), custom_call_target="tpu_custom_call", output_to_operand_aliasing={{}: (3, {})} | custom-call | flops 402653184 | bytes 3145728 | tf_op jit(solution)/shard_map/pallas_call | solution.py:194
  109.5 1.7 %collective-permute-done.3.far_ref = bf16[8,32,1024]{2,1,0:T(8,128)(2,1)S(1)} collective-permute-done((bf16[8,32,1024]{2,1,0:T(8,128)(2,1)S(1)}, bf16[8,32,1024]{2,1,0:T(8,128)(2,1)S(1)}, u32[]{:S(2)}, u32[]{:S(2)}) %collective-permute-start.3) | collective-permute-done | bytes 524320 | tf_op jit(solution)/shard_map/ppermute | solution.py:225
  111.2 1.3 %shard_map.50 = bf16[64,32,1024]{2,1,0:T(8,128)(2,1)} custom-call(bf16[8,5,256,256]{3,2,1,0:T(8,128)(2,1)S(1)} %banded.1.matrix_ref, f32[64,32,1024]{2,1,0:T(8,128)S(1)} %shard_map.47.part_ref, bf16[8,32,1024]{2,1,0:T(8,128)(2,1)S(1)} %collective-permute-done.3.far_ref, bf16[64,32,1024]{2,1,0:T(8,128)(2,1)} %shard_map.49.refs_0_), custom_call_target="tpu_custom_call", output_to_operand_aliasing={{}: (3, {})} | custom-call | flops 134217728 | bytes 1048576 | tf_op jit(solution)/shard_map/pallas_call | solution.py:194
  (16 shorter events, 0.1 us)
Async XLA Ops:
  0.0 67.1 %copy-start.6 = (bf16[8,8,8,129]{3,2,1,0:T(8,128)(2,1)S(1)}, bf16[8,8,8,129]{3,2,1,0:T(8,128)(2,1)}, u32[]{:S(2)}) copy-start(bf16[8,8,8,129]{3,2,1,0:T(8,128)(2,1)} %param.5) | copy-start | bytes 396292
  0.0 55.1 %collective-permute-start = (bf16[64,32,1024]{2,1,0:T(8,128)(2,1)}, bf16[64,32,1024]{2,1,0:T(8,128)(2,1)}, u32[]{:S(2)}, u32[]{:S(2)}) collective-permute-start(bf16[64,32,1024]{2,1,0:T(8,128)(2,1)} %first_ref.1), channel_id=1, source_target_pairs={{0,254},{1,3},{2,0},{3,5},{4,2},{5,7},{6,4},{7,9},{8,6},{9,11},{10... | collective-permute-start | bytes 12582920 | tf_op jit(solution)/shard_map/ppermute | solution.py:219
  8.8 46.3 %collective-permute-start.2 = (bf16[64,32,1024]{2,1,0:T(8,128)(2,1)}, bf16[64,32,1024]{2,1,0:T(8,128)(2,1)S(1)}, u32[]{:S(2)}, u32[]{:S(2)}) collective-permute-start(bf16[64,32,1024]{2,1,0:T(8,128)(2,1)} %first_ref.1), channel_id=1, source_target_pairs={{0,1},{1,0},{2,3},{3,2},{4,5},{5,4},{6,7},{7,6},{8,9},{9,8},{10,11... | collective-permute-start | bytes 12582920 | tf_op jit(solution)/shard_map/ppermute | solution.py:220
  55.1 39.2 %collective-permute-start.1 = (bf16[64,32,1024]{2,1,0:T(8,128)(2,1)}, bf16[64,32,1024]{2,1,0:T(8,128)(2,1)}, u32[]{:S(2)}, u32[]{:S(2)}) collective-permute-start(bf16[64,32,1024]{2,1,0:T(8,128)(2,1)} %collective-permute-done.first_ref), channel_id=1, source_target_pairs={{0,1},{1,0},{2,3},{3,2},{4,5},{5,4},{6,7},{7,6},{8,9},{9,8},{10,11... | collective-permute-start | bytes 12582920 | tf_op jit(solution)/shard_map/ppermute | solution.py:227
  55.1 9.7 %copy-start.2 = (bf16[64,32,1024]{2,1,0:T(8,128)(2,1)}, bf16[64,32,1024]{2,1,0:T(8,128)(2,1)S(1)}, u32[]{:S(2)}) copy-start(bf16[64,32,1024]{2,1,0:T(8,128)(2,1)S(1)} %collective-permute-done.2.second_ref) | copy-start | bytes 12582916
  56.8 44.8 %collective-permute-start.5 = (bf16[32,32,1024]{2,1,0:T(8,128)(2,1)}, bf16[32,32,1024]{2,1,0:T(8,128)(2,1)S(1)}, u32[]{:S(2)}, u32[]{:S(2)}) collective-permute-start(bf16[32,32,1024]{2,1,0:T(8,128)(2,1)} %slice.14), channel_id=1, source_target_pairs={{0,255},{1,2},{2,1},{3,4},{4,3},{5,6},{6,5},{7,8},{8,7},{9,10},{10... | collective-permute-start | bytes 6291464 | tf_op jit(solution)/shard_map/ppermute | solution.py:225
  66.1 39.6 %collective-permute-start.4 = (bf16[24,32,1024]{2,1,0:T(8,128)(2,1)}, bf16[24,32,1024]{2,1,0:T(8,128)(2,1)}, u32[]{:S(2)}, u32[]{:S(2)}) collective-permute-start(bf16[24,32,1024]{2,1,0:T(8,128)(2,1)} %slice.13), channel_id=1, source_target_pairs={{0,255},{1,2},{2,1},{3,4},{4,3},{5,6},{6,5},{7,8},{8,7},{9,10},{10... | collective-permute-start | bytes 4718600 | tf_op jit(solution)/shard_map/ppermute | solution.py:225
  67.3 6.6 %copy-start.4 = (bf16[64,64]{1,0:T(8,128)(2,1)S(1)}, bf16[64,64]{1,0:T(8,128)(2,1)}, u32[]{:S(2)}) copy-start(bf16[64,64]{1,0:T(8,128)(2,1)} %weight_ref.1) | copy-start | bytes 24580
  67.3 6.6 %copy-start.5 = (f32[64]{0:T(128)S(1)}, f32[64]{0:T(128)}, u32[]{:S(2)}) copy-start(f32[64]{0:T(128)} %bias_ref.1) | copy-start | bytes 772
  73.9 2.2 %copy-start = (bf16[64,32,1024]{2,1,0:T(8,128)(2,1)S(1)}, bf16[64,32,1024]{2,1,0:T(8,128)(2,1)}, u32[]{:S(2)}) copy-start(bf16[64,32,1024]{2,1,0:T(8,128)(2,1)} %first_ref.1) | copy-start | bytes 12582916
  76.1 5.0 %copy-start.3 = (bf16[64,32,1024]{2,1,0:T(8,128)(2,1)S(1)}, bf16[64,32,1024]{2,1,0:T(8,128)(2,1)}, u32[]{:S(2)}) copy-start(bf16[64,32,1024]{2,1,0:T(8,128)(2,1)} %copy-done.2) | copy-start | bytes 12582916
  81.0 9.7 %copy-start.1 = (bf16[64,32,1024]{2,1,0:T(8,128)(2,1)S(1)}, bf16[64,32,1024]{2,1,0:T(8,128)(2,1)}, u32[]{:S(2)}) copy-start(bf16[64,32,1024]{2,1,0:T(8,128)(2,1)} %first_ref.1) | copy-start | bytes 12582916
  81.1 30.2 %collective-permute-start.3 = (bf16[8,32,1024]{2,1,0:T(8,128)(2,1)S(1)}, bf16[8,32,1024]{2,1,0:T(8,128)(2,1)S(1)}, u32[]{:S(2)}, u32[]{:S(2)}) collective-permute-start(bf16[8,32,1024]{2,1,0:T(8,128)(2,1)S(1)} %slice.12), channel_id=1, source_target_pairs={{0,255},{1,2},{2,1},{3,4},{4,3},{5,6},{6,5},{7,8},{8,7},{9,10},{10... | collective-permute-start | bytes 1572872 | tf_op jit(solution)/shard_map/ppermute | solution.py:225

commit v3 on v2

--- a/solution.py
+++ b/solution.py
@@ -8,7 +8,7 @@
 from jax.sharding import PartitionSpec as P
 
 FAR, RING_TWIN, OWN, TWIN, RING = range(5)
-FAR_CHUNKS = (4, 3, 1)
+FAR_CHUNKS = (4, 3)
 WHOLE = pl.BlockSpec(memory_space=pltpu.VMEM)
 GRANT = pltpu.CompilerParams(vmem_limit_bytes=16 * 2**20)
 
@@ -147,33 +147,41 @@
     )(matrices, first, second, part)
 
 
-def last_kernel(start, count, matrix_ref, part_ref, far_ref, *refs):
+def last_kernel(start, count, cuts, matrix_ref, part_ref, *refs):
     out_ref, ready_ref, sems = refs[-3:]
     width = ready_ref.shape[0] // count
     rows, columns = ready_ref.shape[1:]
-    tile = columns // 2
+    edges = [0, columns // 2, columns] if cuts is None else cuts
+    tiles = list(zip(edges, edges[1:]))
+
+    def far(g, t):
+        lanes = slice(*tiles[t])
+        if cuts is None:
+            return refs[0][pl.ds(g * width, width), :, lanes]
+        if t == 0:
+            return refs[0][...]
+        return refs[2 * t - 1][...] + refs[2 * t][...]
 
     def copy(g, t):
-        lanes = pl.ds(t * tile, tile)
+        lanes = pl.ds(tiles[t][0], tiles[t][1] - tiles[t][0])
         return pltpu.make_async_copy(
             ready_ref.at[pl.ds(g * width, width), :, lanes],
             out_ref.at[pl.ds((start + g) * width, width), :, lanes],
-            sems.at[2 * g + t],
+            sems.at[len(tiles) * g + t],
         )
 
     def group(g):
-        here = pl.ds(g * width, width)
-        for t in range(2):
-            lanes = slice(t * tile, (t + 1) * tile)
+        for t, (first, last) in enumerate(tiles):
+            lanes = slice(first, last)
             total = jnp.dot(
                 matrix_ref[start + g, FAR],
-                far_ref[here, :, lanes].reshape(width * rows, tile),
+                far(g, t).reshape(width * rows, last - first),
                 preferred_element_type=jnp.float32,
             )
             total = part_ref[pl.ds((start + g) * width, width), :, lanes] + total.reshape(
-                width, rows, tile
+                width, rows, last - first
             )
-            ready_ref[here, :, lanes] = jax.nn.gelu(total).astype(jnp.bfloat16)
+            ready_ref[pl.ds(g * width, width), :, lanes] = jax.nn.gelu(total).astype(jnp.bfloat16)
             copy(g, t).start()
 
     if count == 1:
@@ -181,35 +189,51 @@
     else:
         pl.loop(0, count)(group)
     for g in range(count):
-        for t in range(2):
+        for t in range(len(tiles)):
             copy(g, t).wait()
 
 
-def finish(matrices, part, far, out, start, count):
+def finish(matrices, part, fars, out, start, count, cuts):
     groups, _, lanes, _ = matrices.shape
     channels, rows, columns = part.shape
     width = channels // groups
     given = [] if out is None else [out]
     whole = pl.BlockSpec(memory_space=pl.ANY)
-    return pl.pallas_call(
-        functools.partial(last_kernel, start, count),
-        in_specs=[WHOLE] * 3 + [whole] * len(given),
+    size = count * width * rows * columns
+    return pl.pallas_call(
+        functools.partial(last_kernel, start, count, cuts),
+        in_specs=[WHOLE] * (2 + len(fars)) + [whole] * len(given),
         out_specs=whole,
         out_shape=jax.ShapeDtypeStruct(part.shape, jnp.bfloat16),
-        input_output_aliases={3: 0} if given else {},
+        input_output_aliases={2 + len(fars): 0} if given else {},
         scratch_shapes=[
             pltpu.VMEM((count * width, rows, columns), jnp.bfloat16),
-            pltpu.SemaphoreType.DMA((2 * count,)),
+            pltpu.SemaphoreType.DMA((3 * count,)),
         ],
         compiler_params=GRANT,
         cost_estimate=pl.CostEstimate(
-            flops=2 * lanes * far.size, bytes_accessed=4 * far.size, transcendentals=far.size
+            flops=2 * lanes * size, bytes_accessed=4 * size, transcendentals=size
         ),
-    )(matrices, part, far, *given)
+    )(matrices, part, *fars, *given)
+
+
+def relay_hops(devices):
+    if devices != 256:
+        return [], [], []
+
+    def strip(x, z, y, core):
+        return ((x % 4 * 8 + z % 8) * 4 + y) * 2 + core
+
+    paths = []
+    for x in range(4):
+        low, high = strip(x - 1, 7, 3, 1), strip(x, 0, 0, 0)
+        paths.append([low, strip(x - 1, 6, 3, 1), strip(x, 6, 0, 1), high])
+        paths.append([high, strip(x, 1, 0, 1), strip(x - 1, 1, 3, 1), low])
+    return tuple([tuple(path[i : i + 2]) for path in paths] for i in range(3))
 
 
 def local(features, row_kernel, mix_weight, channel_bias):
-    strip_rows = features.shape[1]
+    strip_rows, columns = features.shape[1:]
     width = row_kernel.shape[1]
     devices = lax.axis_size("strip")
     odd = lax.rem(lax.axis_index("strip"), 2).reshape(1)
@@ -224,6 +248,17 @@
         piece = twin[start * width : (start + count) * width]
         fars.append(lax.ppermute(piece, "strip", far_route))
         start += count
+    end = twin[start * width :]
+    cuts = [0, 5 * columns // 8, columns]
+    ends = [lax.ppermute(end[:, :, : cuts[1]], "strip", far_route)]
+    piece = end[:, :, cuts[1] :]
+    hops = relay_hops(devices)
+    relayed = [target for _, target in hops[2]]
+    route = [pair for pair in far_route if pair[1] not in relayed]
+    ends.append(lax.ppermute(piece, "strip", route))
+    for hop in hops:
+        piece = lax.ppermute(piece, "strip", hop)
+    ends.append(piece)
     ring_twin = lax.ppermute(ring, "strip", twin_route)
     matrices = banded_matrices(row_kernel, odd, strip_rows)
     part = mix(features, mix_weight, channel_bias)
@@ -232,9 +267,9 @@
     out = None
     start = 0
     for far, count in zip(fars, FAR_CHUNKS):
-        out = finish(matrices, part, far, out, start, count)
+        out = finish(matrices, part, [far], out, start, count, None)
         start += count
-    return out
+    return finish(matrices, part, ends, out, start, 1, cuts)
 
 
 def solution(mesh):

time: 113 us -> 114 us (level)
  starting transfers between devices: 24.1 us -> 28.3 us
  waiting for transfers between devices: 49.2 us -> 46.4 us
  local copies, waits for them, and re-layouts: 11.8 us -> 10.6 us
    ppermute x0 -> x5, starting transfers between devices: none -> 10.5 us  [the longest x1 6.32 us: local(): ends = [lax.ppermute(end[:, :, :cuts[1]], 'strip', far_route)]]
    ppermute x3 -> x2, starting transfers between devices: 15.3 us -> 8.96 us  [local(): fars.append(lax.ppermute(piece, 'strip', far_route))]
    ppermute x3 -> x2, waiting for transfers between devices: 2.91 us -> 0.01 us  [local(): fars.append(lax.ppermute(piece, 'strip', far_route))]
    unnamed x14 -> x12, local copies, waits for them, and re-layouts: 2.21 us -> 0.03 us
    slice x3 -> x2, local copies, waits for them, and re-layouts: 3 us -> 2.99 us  [local(): piece = twin[start * width:(start + count) * width]]
  transfers between devices with their start and end apart: 6 -> 10, of which waited for: 3 -> 1; matrix products, arithmetic and copies ran while one was open for 9% -> 10% of each run, Pallas kernels for 23% -> 23%
where the time goes in v3:
time: 114 us; the launch traced here: 113 us
  waiting for transfers between devices  46.4 us (41%)
  starting transfers between devices  28.3 us (25%)
  Pallas kernels  27.2 us (24%)
  local copies, waits for them, and re-layouts  10.6 us (9%)
    ppermute x1, waiting for transfers between devices, local(): ring = lax.ppermute(features, 'strip', ring_route)  46.3 us
    pallas_call x2, Pallas kernels, add_pair(): pl.pallas_call(functools.partial(pair_kernel, first_role, second_role), g...  10.9 us
    ppermute x2, starting transfers between devices, local(): fars.append(lax.ppermute(piece, 'strip', far_route))  8.96 us
    ppermute x1, starting transfers between devices, local(): ring = lax.ppermute(features, 'strip', ring_route)  8.79 us
    pallas_call x3, Pallas kernels, finish(): pl.pallas_call(functools.partial(last_kernel, start, count, cuts), in_spe...  8 us
    reshape x3, local copies, waits for them, and re-layouts, banded_matrices(): jnp.transpose(rows, (0, 3, 1, 2, 4))  6.6 us
    ppermute x1, starting transfers between devices, local(): ends = [lax.ppermute(end[:, :, :cuts[1]], 'strip', far_route)]  6.32 us
    pallas_call x1, Pallas kernels, mix(): pl.pallas_call(mix_kernel, grid=(rows // part, 2), in_specs=[pl.BlockSpec...  4.95 us
  transfers between devices with their start and end apart: 10, of which 1 were waited for; matrix products, arithmetic and copies ran while one was open for 10% of the time, Pallas kernels for 23%

profile of v3, /device:TPU:0, one launch (start us, length us, event | category | flops | bytes accessed | tf_op | source)
XLA Modules:
  0.0 112.8 jit_solution(15014315918304212642)
XLA Ops:
  0.0 8.8 %collective-permute-start = (bf16[64,32,1024]{2,1,0:T(8,128)(2,1)}, bf16[64,32,1024]{2,1,0:T(8,128)(2,1)}, u32[]{:S(2)}, u32[]{:S(2)}) collective-permute-start(bf16[64,32,1024]{2,1,0:T(8,128)(2,1)} %first_ref.1), channel_id=1, source_target_pairs={{0,254},{1,3},{2,0},{3,5},{4,2},{5,7},{6,4},{7,9},{8,6},{9,11},{10... | collective-permute-start | bytes 12582920 | tf_op jit(solution)/shard_map/ppermute | solution.py:243
  8.8 46.3 %collective-permute-done.first_ref = bf16[64,32,1024]{2,1,0:T(8,128)(2,1)} collective-permute-done((bf16[64,32,1024]{2,1,0:T(8,128)(2,1)}, bf16[64,32,1024]{2,1,0:T(8,128)(2,1)}, u32[]{:S(2)}, u32[]{:S(2)}) %collective-permute-start) | collective-permute-done | bytes 4194336 | tf_op jit(solution)/shard_map/ppermute | solution.py:243
  55.1 1.7 %slice.22 = bf16[32,32,1024]{2,1,0:T(8,128)(2,1)} slice(bf16[64,32,1024]{2,1,0:T(8,128)(2,1)S(1)} %collective-permute-done.2.second_ref), slice={[0:32], [0:32], [0:1024]} | slice | bytes 4194304 | tf_op jit(solution)/shard_map/slice | solution.py:248
  56.8 8.0 %collective-permute-start.9 = (bf16[32,32,1024]{2,1,0:T(8,128)(2,1)}, bf16[32,32,1024]{2,1,0:T(8,128)(2,1)S(1)}, u32[]{:S(2)}, u32[]{:S(2)}) collective-permute-start(bf16[32,32,1024]{2,1,0:T(8,128)(2,1)} %slice.22), channel_id=1, source_target_pairs={{0,255},{1,2},{2,1},{3,4},{4,3},{5,6},{6,5},{7,8},{8,7},{9,10},{10... | collective-permute-start | bytes 6291464 | tf_op jit(solution)/shard_map/ppermute | solution.py:249
  64.9 1.3 %slice.21 = bf16[24,32,1024]{2,1,0:T(8,128)(2,1)} slice(bf16[64,32,1024]{2,1,0:T(8,128)(2,1)S(1)} %collective-permute-done.2.second_ref), slice={[32:56], [0:32], [0:1024]} | slice | bytes 3145728 | tf_op jit(solution)/shard_map/slice | solution.py:248
  66.2 0.9 collective-permute-start.8
  67.1 0.1 pad_convert_fusion
  67.3 1.7 %reshape.20 = f32[8,8,8,6,32]{4,3,2,1,0:T(8,128)} reshape(f32[8,8,8,192]{3,2,1,0:T(8,128)S(1)} %pad_convert_fusion) | data formatting | bytes 786432 | tf_op jit(solution)/shard_map/reshape | solution.py:47
  69.0 3.0 %copy.10 = f32[8,6,8,8,32]{4,3,2,1,0:T(8,128)} copy(f32[8,6,8,8,32]{4,1,3,2,0:T(8,128)} %bitcast.6) | data formatting | bytes 786432 | tf_op jit(solution)/shard_map/reshape | solution.py:47
  72.0 1.9 %reshape.17.rows_ref = f32[8,6,8,256]{3,2,1,0:T(8,128)S(1)} reshape(f32[8,6,8,8,32]{4,3,2,1,0:T(8,128)} %copy.10) | data formatting | bytes 786432 | tf_op jit(solution)/shard_map/reshape | solution.py:47
  73.9 0.0 copy-start
  73.9 3.4 %banded.1.matrix_ref = bf16[8,5,256,256]{3,2,1,0:T(8,128)(2,1)S(1)} custom-call(s32[1]{0:T(128)} %bitcast.odd_ref, f32[8,6,8,256]{3,2,1,0:T(8,128)S(1)} %reshape.17.rows_ref), custom_call_target="tpu_custom_call" | custom-call | flops 1000000000 | bytes 4000000 | tf_op jit(solution)/shard_map/banded/pallas_call | solution.py:48
  77.3 1.0 slice.20
  78.2 1.6 %collective-permute-start.5 = (bf16[8,32,384]{2,1,0:T(8,128)(2,1)S(1)}, bf16[8,32,384]{2,1,0:T(8,128)(2,1)S(1)}, u32[]{:S(2)}, u32[]{:S(2)}) collective-permute-start(bf16[8,32,384]{2,1,0:T(8,128)(2,1)S(1)} %slice.20), channel_id=1, source_target_pairs={{255,247},{0,9},{63,55},{64,73},{127,119},{128,137},{191,183},{192... | collective-permute-start | bytes 589832 | tf_op jit(solution)/shard_map/ppermute | solution.py:260
  79.8 5.0 %mix.1.part_ref = f32[64,32,1024]{2,1,0:T(8,128)S(1)} custom-call(f32[64]{0:T(128)S(1)} %copy-done.4, bf16[64,64]{1,0:T(8,128)(2,1)S(1)} %copy-done.3, bf16[64,32,1024]{2,1,0:T(8,128)(2,1)S(1)} %copy-done), custom_call_target="tpu_custom_call" | custom-call | flops 2147483648 | bytes 12582912 | tf_op jit(solution)/shard_map/mix/pallas_call | solution.py:96
  84.8 6.3 %collective-permute-start.3 = (bf16[8,32,640]{2,1,0:T(8,128)(2,1)S(1)}, bf16[8,32,640]{2,1,0:T(8,128)(2,1)S(1)}, u32[]{:S(2)}, u32[]{:S(2)}) collective-permute-start(bf16[8,32,640]{2,1,0:T(8,128)(2,1)S(1)} %slice.19), channel_id=1, source_target_pairs={{0,255},{1,2},{2,1},{3,4},{4,3},{5,6},{6,5},{7,8},{8,7},{9,10},{10... | collective-permute-start | bytes 983048 | tf_op jit(solution)/shard_map/ppermute | solution.py:253
  91.2 0.7 collective-permute-start.6
  91.8 3.6 %shard_map.46.part_ref = f32[64,32,1024]{2,1,0:T(8,128)S(1)} custom-call(bf16[8,5,256,256]{3,2,1,0:T(8,128)(2,1)S(1)} %banded.1.matrix_ref, bf16[64,32,1024]{2,1,0:T(8,128)(2,1)S(1)} %copy-done, bf16[64,32,1024]{2,1,0:T(8,128)(2,1)S(1)} %copy-done.2, f32[64,32,1024]{2,1,0:T(8,128)S(1)} %mix.1.part_ref), custom_call_target="tpu_custom_call", output_to_operand_aliasing={{}: (3, {})} | custom-call | flops 2147483648 | bytes 8388608 | tf_op jit(solution)/shard_map/pallas_call | solution.py:136
  95.4 0.7 collective-permute-start.4
  96.1 1.3 %collective-permute-start.7 = (bf16[8,32,384]{2,1,0:T(8,128)(2,1)S(1)}, bf16[8,32,384]{2,1,0:T(8,128)(2,1)S(1)}, u32[]{:S(2)}, u32[]{:S(2)}) collective-permute-start(bf16[8,32,384]{2,1,0:T(8,128)(2,1)S(1)} %collective-permute-done.6), channel_id=1, source_target_pairs={{49,0},{207,255},{113,64},{15,63},{177,128},{79,127},{241,192},{14... | collective-permute-start | bytes 589832 | tf_op jit(solution)/shard_map/ppermute | solution.py:260
  97.4 7.3 %shard_map.47.part_ref = f32[64,32,1024]{2,1,0:T(8,128)S(1)} custom-call(bf16[8,5,256,256]{3,2,1,0:T(8,128)(2,1)S(1)} %banded.1.matrix_ref, bf16[64,32,1024]{2,1,0:T(8,128)(2,1)} %collective-permute-done.first_ref, bf16[64,32,1024]{2,1,0:T(8,128)(2,1)} %collective-permute-done.1.second_ref, ...), custom_call_target="tpu_custom_call", output_to_operand_aliasing={{}: (3, {})} | custom-call | flops 2147483648 | bytes 8388608 | tf_op jit(solution)/shard_map/pallas_call | solution.py:136
  104.7 2.9 %shard_map.48.refs_1_ = bf16[64,32,1024]{2,1,0:T(8,128)(2,1)} custom-call(bf16[8,5,256,256]{3,2,1,0:T(8,128)(2,1)S(1)} %banded.1.matrix_ref, f32[64,32,1024]{2,1,0:T(8,128)S(1)} %shard_map.47.part_ref, bf16[32,32,1024]{2,1,0:T(8,128)(2,1)S(1)} %collective-permute-done.9.refs_0_), custom_call_target="tpu_custom_call" | custom-call | flops 536870912 | bytes 4194304 | tf_op jit(solution)/shard_map/pallas_call | solution.py:203
  107.7 3.8 %shard_map.49.refs_3_ = bf16[64,32,1024]{2,1,0:T(8,128)(2,1)} custom-call(bf16[8,5,256,256]{3,2,1,0:T(8,128)(2,1)S(1)} %banded.1.matrix_ref, f32[64,32,1024]{2,1,0:T(8,128)S(1)} %shard_map.47.part_ref, bf16[24,32,1024]{2,1,0:T(8,128)(2,1)} %collective-permute-done.8.refs_0_, bf16[64,32,1024]{2,1,0:T(8,128)(2,1)} %shard_map.48.refs_1_), custom_call_target="tpu_custom_call", output_to_operand_aliasing={{}: (3, {})} | custom-call | flops 402653184 | bytes 3145728 | tf_op jit(solution)/shard_map/pallas_call | solution.py:203
  111.5 1.3 %shard_map.50 = bf16[64,32,1024]{2,1,0:T(8,128)(2,1)} custom-call(bf16[8,5,256,256]{3,2,1,0:T(8,128)(2,1)S(1)} %banded.1.matrix_ref, f32[64,32,1024]{2,1,0:T(8,128)S(1)} %shard_map.47.part_ref, bf16[8,32,640]{2,1,0:T(8,128)(2,1)S(1)} %collective-permute-done.3.refs_0_, ...), custom_call_target="tpu_custom_call", output_to_operand_aliasing={{}: (5, {})} | custom-call | flops 134217728 | bytes 1048576 | tf_op jit(solution)/shard_map/pallas_call | solution.py:203
  (23 shorter events, 0.1 us)
Async XLA Ops:
  0.0 67.1 %copy-start.5 = (bf16[8,8,8,129]{3,2,1,0:T(8,128)(2,1)S(1)}, bf16[8,8,8,129]{3,2,1,0:T(8,128)(2,1)}, u32[]{:S(2)}) copy-start(bf16[8,8,8,129]{3,2,1,0:T(8,128)(2,1)} %param.5) | copy-start | bytes 396292
  0.0 55.1 %collective-permute-start = (bf16[64,32,1024]{2,1,0:T(8,128)(2,1)}, bf16[64,32,1024]{2,1,0:T(8,128)(2,1)}, u32[]{:S(2)}, u32[]{:S(2)}) collective-permute-start(bf16[64,32,1024]{2,1,0:T(8,128)(2,1)} %first_ref.1), channel_id=1, source_target_pairs={{0,254},{1,3},{2,0},{3,5},{4,2},{5,7},{6,4},{7,9},{8,6},{9,11},{10... | collective-permute-start | bytes 12582920 | tf_op jit(solution)/shard_map/ppermute | solution.py:243
  8.8 46.3 %collective-permute-start.2 = (bf16[64,32,1024]{2,1,0:T(8,128)(2,1)}, bf16[64,32,1024]{2,1,0:T(8,128)(2,1)S(1)}, u32[]{:S(2)}, u32[]{:S(2)}) collective-permute-start(bf16[64,32,1024]{2,1,0:T(8,128)(2,1)} %first_ref.1), channel_id=1, source_target_pairs={{0,1},{1,0},{2,3},{3,2},{4,5},{5,4},{6,7},{7,6},{8,9},{9,8},{10,11... | collective-permute-start | bytes 12582920 | tf_op jit(solution)/shard_map/ppermute | solution.py:244
  55.1 41.0 %collective-permute-start.1 = (bf16[64,32,1024]{2,1,0:T(8,128)(2,1)}, bf16[64,32,1024]{2,1,0:T(8,128)(2,1)}, u32[]{:S(2)}, u32[]{:S(2)}) collective-permute-start(bf16[64,32,1024]{2,1,0:T(8,128)(2,1)} %collective-permute-done.first_ref), channel_id=1, source_target_pairs={{0,1},{1,0},{2,3},{3,2},{4,5},{5,4},{6,7},{7,6},{8,9},{9,8},{10,11... | collective-permute-start | bytes 12582920 | tf_op jit(solution)/shard_map/ppermute | solution.py:262
  55.1 9.7 %copy-start.1 = (bf16[64,32,1024]{2,1,0:T(8,128)(2,1)}, bf16[64,32,1024]{2,1,0:T(8,128)(2,1)S(1)}, u32[]{:S(2)}) copy-start(bf16[64,32,1024]{2,1,0:T(8,128)(2,1)S(1)} %collective-permute-done.2.second_ref) | copy-start | bytes 12582916
  56.8 47.9 %collective-permute-start.9 = (bf16[32,32,1024]{2,1,0:T(8,128)(2,1)}, bf16[32,32,1024]{2,1,0:T(8,128)(2,1)S(1)}, u32[]{:S(2)}, u32[]{:S(2)}) collective-permute-start(bf16[32,32,1024]{2,1,0:T(8,128)(2,1)} %slice.22), channel_id=1, source_target_pairs={{0,255},{1,2},{2,1},{3,4},{4,3},{5,6},{6,5},{7,8},{8,7},{9,10},{10... | collective-permute-start | bytes 6291464 | tf_op jit(solution)/shard_map/ppermute | solution.py:249
  66.2 41.5 %collective-permute-start.8 = (bf16[24,32,1024]{2,1,0:T(8,128)(2,1)}, bf16[24,32,1024]{2,1,0:T(8,128)(2,1)}, u32[]{:S(2)}, u32[]{:S(2)}) collective-permute-start(bf16[24,32,1024]{2,1,0:T(8,128)(2,1)} %slice.21), channel_id=1, source_target_pairs={{0,255},{1,2},{2,1},{3,4},{4,3},{5,6},{6,5},{7,8},{8,7},{9,10},{10... | collective-permute-start | bytes 4718600 | tf_op jit(solution)/shard_map/ppermute | solution.py:249
  72.0 7.8 %copy-start.3 = (bf16[64,64]{1,0:T(8,128)(2,1)S(1)}, bf16[64,64]{1,0:T(8,128)(2,1)}, u32[]{:S(2)}) copy-start(bf16[64,64]{1,0:T(8,128)(2,1)} %weight_ref.1) | copy-start | bytes 24580
  72.0 7.8 %copy-start.4 = (f32[64]{0:T(128)S(1)}, f32[64]{0:T(128)}, u32[]{:S(2)}) copy-start(f32[64]{0:T(128)} %bias_ref.1) | copy-start | bytes 772
  73.9 5.9 %copy-start = (bf16[64,32,1024]{2,1,0:T(8,128)(2,1)S(1)}, bf16[64,32,1024]{2,1,0:T(8,128)(2,1)}, u32[]{:S(2)}) copy-start(bf16[64,32,1024]{2,1,0:T(8,128)(2,1)} %first_ref.1) | copy-start | bytes 12582916
  78.2 6.6 %copy-start.2 = (bf16[64,32,1024]{2,1,0:T(8,128)(2,1)S(1)}, bf16[64,32,1024]{2,1,0:T(8,128)(2,1)}, u32[]{:S(2)}) copy-start(bf16[64,32,1024]{2,1,0:T(8,128)(2,1)} %copy-done.1) | copy-start | bytes 12582916
  78.2 12.9 %collective-permute-start.5 = (bf16[8,32,384]{2,1,0:T(8,128)(2,1)S(1)}, bf16[8,32,384]{2,1,0:T(8,128)(2,1)S(1)}, u32[]{:S(2)}, u32[]{:S(2)}) collective-permute-start(bf16[8,32,384]{2,1,0:T(8,128)(2,1)S(1)} %slice.20), channel_id=1, source_target_pairs={{255,247},{0,9},{63,55},{64,73},{127,119},{128,137},{191,183},{192... | collective-permute-start | bytes 589832 | tf_op jit(solution)/shard_map/ppermute | solution.py:260
  84.8 26.7 %collective-permute-start.3 = (bf16[8,32,640]{2,1,0:T(8,128)(2,1)S(1)}, bf16[8,32,640]{2,1,0:T(8,128)(2,1)S(1)}, u32[]{:S(2)}, u32[]{:S(2)}) collective-permute-start(bf16[8,32,640]{2,1,0:T(8,128)(2,1)S(1)} %slice.19), channel_id=1, source_target_pairs={{0,255},{1,2},{2,1},{3,4},{4,3},{5,6},{6,5},{7,8},{8,7},{9,10},{10... | collective-permute-start | bytes 983048 | tf_op jit(solution)/shard_map/ppermute | solution.py:253
  91.2 4.3 %collective-permute-start.6 = (bf16[8,32,384]{2,1,0:T(8,128)(2,1)S(1)}, bf16[8,32,384]{2,1,0:T(8,128)(2,1)S(1)}, u32[]{:S(2)}, u32[]{:S(2)}) collective-permute-start(bf16[8,32,384]{2,1,0:T(8,128)(2,1)S(1)} %collective-permute-done.5), channel_id=1, source_target_pairs={{247,49},{9,207},{55,113},{73,15},{119,177},{137,79},{183,241},{20... | collective-permute-start | bytes 589832 | tf_op jit(solution)/shard_map/ppermute | solution.py:260
  95.4 16.1 %collective-permute-start.4 = (bf16[8,32,384]{2,1,0:T(8,128)(2,1)S(1)}, bf16[8,32,384]{2,1,0:T(8,128)(2,1)S(1)}, u32[]{:S(2)}, u32[]{:S(2)}) collective-permute-start(bf16[8,32,384]{2,1,0:T(8,128)(2,1)S(1)} %slice.20), channel_id=1, source_target_pairs={{1,2},{2,1},{3,4},{4,3},{5,6},{6,5},{7,8},{8,7},{9,10},{10,9},{11,... | collective-permute-start | bytes 589832 | tf_op jit(solution)/shard_map/ppermute | solution.py:258
  96.1 15.4 %collective-permute-start.7 = (bf16[8,32,384]{2,1,0:T(8,128)(2,1)S(1)}, bf16[8,32,384]{2,1,0:T(8,128)(2,1)S(1)}, u32[]{:S(2)}, u32[]{:S(2)}) collective-permute-start(bf16[8,32,384]{2,1,0:T(8,128)(2,1)S(1)} %collective-permute-done.6), channel_id=1, source_target_pairs={{49,0},{207,255},{113,64},{15,63},{177,128},{79,127},{241,192},{14... | collective-permute-start | bytes 589832 | tf_op jit(solution)/shard_map/ppermute | solution.py:260

commit v4 on v3

--- a/solution.py
+++ b/solution.py
@@ -9,6 +9,7 @@
 
 FAR, RING_TWIN, OWN, TWIN, RING = range(5)
 FAR_CHUNKS = (4, 3)
+RELAY_PLANES = ((5, 1), (6, 2))
 WHOLE = pl.BlockSpec(memory_space=pltpu.VMEM)
 GRANT = pltpu.CompilerParams(vmem_limit_bytes=16 * 2**20)
 
@@ -217,7 +218,7 @@
     )(matrices, part, *fars, *given)
 
 
-def relay_hops(devices):
+def relay_hops(devices, up_plane, down_plane):
     if devices != 256:
         return [], [], []
 
@@ -227,8 +228,8 @@
     paths = []
     for x in range(4):
         low, high = strip(x - 1, 7, 3, 1), strip(x, 0, 0, 0)
-        paths.append([low, strip(x - 1, 6, 3, 1), strip(x, 6, 0, 1), high])
-        paths.append([high, strip(x, 1, 0, 1), strip(x - 1, 1, 3, 1), low])
+        paths.append([low, strip(x - 1, up_plane, 3, 1), strip(x, up_plane, 0, 1), high])
+        paths.append([high, strip(x, down_plane, 0, 1), strip(x - 1, down_plane, 3, 1), low])
     return tuple([tuple(path[i : i + 2]) for path in paths] for i in range(3))
 
 
@@ -249,20 +250,22 @@
         fars.append(lax.ppermute(piece, "strip", far_route))
         start += count
     end = twin[start * width :]
-    cuts = [0, 5 * columns // 8, columns]
+    cuts = [0, columns // 2, 3 * columns // 4, columns]
     ends = [lax.ppermute(end[:, :, : cuts[1]], "strip", far_route)]
-    piece = end[:, :, cuts[1] :]
-    hops = relay_hops(devices)
-    relayed = [target for _, target in hops[2]]
-    route = [pair for pair in far_route if pair[1] not in relayed]
-    ends.append(lax.ppermute(piece, "strip", route))
-    for hop in hops:
-        piece = lax.ppermute(piece, "strip", hop)
-    ends.append(piece)
+    for t, planes in enumerate(RELAY_PLANES, 1):
+        piece = end[:, :, cuts[t] : cuts[t + 1]]
+        hops = relay_hops(devices, *planes)
+        relayed = [target for _, target in hops[2]]
+        route = [pair for pair in far_route if pair[1] not in relayed]
+        ends.append(lax.ppermute(piece, "strip", route))
+        for hop in hops:
+            piece = lax.ppermute(piece, "strip", hop)
+        ends.append(piece)
     ring_twin = lax.ppermute(ring, "strip", twin_route)
     matrices = banded_matrices(row_kernel, odd, strip_rows)
-    part = mix(features, mix_weight, channel_bias)
-    part = add_pair(matrices, features, OWN, twin, TWIN, part)
+    own = features
+    part = mix(own, mix_weight, channel_bias)
+    part = add_pair(matrices, own, OWN, twin, TWIN, part)
     part = add_pair(matrices, ring, RING, ring_twin, RING_TWIN, part)
     out = None
     start = 0

time: 114 us -> 136 us (1.19)
  local copies, waits for them, and re-layouts: 10.6 us -> 26.2 us
  starting transfers between devices: 28.3 us -> 32 us
  waiting for transfers between devices: 46.4 us -> 48.7 us
    unnamed x12 -> x22, local copies, waits for them, and re-layouts: 0.03 us -> 15.5 us
    ppermute x3 -> x6, starting transfers between devices: 3.52 us -> 6.51 us  [local(): piece = lax.ppermute(piece, 'strip', hop)]
    ppermute x2, waiting for transfers between devices: 0.01 us -> 2.32 us  [local(): fars.append(lax.ppermute(piece, 'strip', far_route))]
  transfers between devices with their start and end apart: 10 -> 14, of which waited for: 1 -> 2; matrix products, arithmetic and copies ran while one was open for 10% -> 8% of each run, Pallas kernels for 23% -> 19%
where the time goes in v4:
time: 136 us; the launch traced here: 134 us
  waiting for transfers between devices  48.7 us (36%)
  starting transfers between devices  32 us (24%)
  Pallas kernels  27.2 us (20%)
  local copies, waits for them, and re-layouts  26.2 us (19%)
    ppermute x1, waiting for transfers between devices, local(): ring = lax.ppermute(features, 'strip', ring_route)  46.3 us
    unnamed x22, local copies, waits for them, and re-layouts  15.5 us
    pallas_call x2, Pallas kernels, add_pair(): pl.pallas_call(functools.partial(pair_kernel, first_role, second_role), g...  10.8 us
    ppermute x1, starting transfers between devices, local(): ring = lax.ppermute(features, 'strip', ring_route)  8.87 us
    ppermute x2, starting transfers between devices, local(): fars.append(lax.ppermute(piece, 'strip', far_route))  8.11 us
    pallas_call x3, Pallas kernels, finish(): pl.pallas_call(functools.partial(last_kernel, start, count, cuts), in_spe...  7.99 us
    ppermute x1, starting transfers between devices, local(): ends = [lax.ppermute(end[:, :, :cuts[1]], 'strip', far_route)]  7.17 us
    reshape x3, local copies, waits for them, and re-layouts, banded_matrices(): jnp.transpose(rows, (0, 3, 1, 2, 4))  6.63 us
  transfers between devices with their start and end apart: 14, of which 2 were waited for; matrix products, arithmetic and copies ran while one was open for 8% of the time, Pallas kernels for 19%

profile of v4, /device:TPU:0, one launch (start us, length us, event | category | flops | bytes accessed | tf_op | source)
XLA Modules:
  0.0 134.4 jit_solution(4168019006032410657)
XLA Ops:
  0.0 8.9 %collective-permute-start = (bf16[64,32,1024]{2,1,0:T(8,128)(2,1)}, bf16[64,32,1024]{2,1,0:T(8,128)(2,1)}, u32[]{:S(2)}, u32[]{:S(2)}) collective-permute-start(bf16[64,32,1024]{2,1,0:T(8,128)(2,1)} %first_ref.1), channel_id=1, source_target_pairs={{0,254},{1,3},{2,0},{3,5},{4,2},{5,7},{6,4},{7,9},{8,6},{9,11},{10... | collective-permute-start | bytes 12582920 | tf_op jit(solution)/shard_map/ppermute | solution.py:244
  8.9 46.3 %collective-permute-done.first_ref = bf16[64,32,1024]{2,1,0:T(8,128)(2,1)} collective-permute-done((bf16[64,32,1024]{2,1,0:T(8,128)(2,1)}, bf16[64,32,1024]{2,1,0:T(8,128)(2,1)}, u32[]{:S(2)}, u32[]{:S(2)}) %collective-permute-start) | collective-permute-done | bytes 4194336 | tf_op jit(solution)/shard_map/ppermute | solution.py:244
  55.2 1.8 %slice.28 = bf16[32,32,1024]{2,1,0:T(8,128)(2,1)} slice(bf16[64,32,1024]{2,1,0:T(8,128)(2,1)S(1)} %collective-permute-done.2.second_ref), slice={[0:32], [0:32], [0:1024]} | slice | bytes 4194304 | tf_op jit(solution)/shard_map/slice | solution.py:249
  57.0 8.0 %collective-permute-start.13 = (bf16[32,32,1024]{2,1,0:T(8,128)(2,1)}, bf16[32,32,1024]{2,1,0:T(8,128)(2,1)S(1)}, u32[]{:S(2)}, u32[]{:S(2)}) collective-permute-start(bf16[32,32,1024]{2,1,0:T(8,128)(2,1)} %slice.28), channel_id=1, source_target_pairs={{0,255},{1,2},{2,1},{3,4},{4,3},{5,6},{6,5},{7,8},{8,7},{9,10},{10... | collective-permute-start | bytes 6291464 | tf_op jit(solution)/shard_map/ppermute | solution.py:250
  65.0 1.3 slice.27
  66.4 5.0 %mix.1.part_ref = f32[64,32,1024]{2,1,0:T(8,128)S(1)} custom-call(f32[64]{0:T(128)S(1)} %copy-done.9, bf16[64,64]{1,0:T(8,128)(2,1)S(1)} %copy-done.8, bf16[64,32,1024]{2,1,0:T(8,128)(2,1)S(1)} %copy-done.4), custom_call_target="tpu_custom_call" | custom-call | flops 2147483648 | bytes 12582912 | tf_op jit(solution)/shard_map/mix/pallas_call | solution.py:97
  71.4 3.3 %copy-done = f32[64,32,1024]{2,1,0:T(8,128)} copy-done((f32[64,32,1024]{2,1,0:T(8,128)}, f32[64,32,1024]{2,1,0:T(8,128)S(1)}, u32[]{:S(2)}) %copy-start) | copy-done | bytes 8388632
  74.7 1.3 collective-permute-start.9
  76.0 1.3 collective-permute-start.5
  77.5 1.7 %reshape.20 = f32[8,8,8,6,32]{4,3,2,1,0:T(8,128)} reshape(f32[8,8,8,192]{3,2,1,0:T(8,128)S(1)} %pad_convert_fusion) | data formatting | bytes 786432 | tf_op jit(solution)/shard_map/reshape | solution.py:48
  79.2 3.1 %copy.10 = f32[8,6,8,8,32]{4,3,2,1,0:T(8,128)} copy(f32[8,6,8,8,32]{4,1,3,2,0:T(8,128)} %bitcast.6) | data formatting | bytes 786432 | tf_op jit(solution)/shard_map/reshape | solution.py:48
  82.2 1.9 %reshape.17.rows_ref = f32[8,6,8,256]{3,2,1,0:T(8,128)S(1)} reshape(f32[8,6,8,8,32]{4,3,2,1,0:T(8,128)} %copy.10) | data formatting | bytes 786432 | tf_op jit(solution)/shard_map/reshape | solution.py:48
  84.1 3.4 %banded.1.matrix_ref = bf16[8,5,256,256]{3,2,1,0:T(8,128)(2,1)S(1)} custom-call(s32[1]{0:T(128)} %bitcast.odd_ref, f32[8,6,8,256]{3,2,1,0:T(8,128)S(1)} %reshape.17.rows_ref), custom_call_target="tpu_custom_call" | custom-call | flops 1000000000 | bytes 4000000 | tf_op jit(solution)/shard_map/banded/pallas_call | solution.py:49
  89.9 3.4 %copy-done.1 = f32[64,32,1024]{2,1,0:T(8,128)S(1)} copy-done((f32[64,32,1024]{2,1,0:T(8,128)S(1)}, f32[64,32,1024]{2,1,0:T(8,128)}, u32[]{:S(2)}) %copy-start.1) | copy-done | bytes 8388632
  93.2 2.2 %copy-done.7 = bf16[64,32,1024]{2,1,0:T(8,128)(2,1)S(1)} copy-done((bf16[64,32,1024]{2,1,0:T(8,128)(2,1)S(1)}, bf16[64,32,1024]{2,1,0:T(8,128)(2,1)}, u32[]{:S(2)}) %copy-start.7) | copy-done | bytes 4194328
  95.4 3.6 %shard_map.46.part_ref = f32[64,32,1024]{2,1,0:T(8,128)S(1)} custom-call(bf16[8,5,256,256]{3,2,1,0:T(8,128)(2,1)S(1)} %banded.1.matrix_ref, bf16[64,32,1024]{2,1,0:T(8,128)(2,1)S(1)} %copy-done.5, bf16[64,32,1024]{2,1,0:T(8,128)(2,1)S(1)} %copy-done.7, f32[64,32,1024]{2,1,0:T(8,128)S(1)} %copy-done.1), custom_call_target="tpu_custom_call", output_to_operand_aliasing={{}: (3, {})} | custom-call | flops 2147483648 | bytes 8388608 | tf_op jit(solution)/shard_map/pallas_call | solution.py:137
  99.0 3.3 %copy-done.2 = f32[64,32,1024]{2,1,0:T(8,128)} copy-done((f32[64,32,1024]{2,1,0:T(8,128)}, f32[64,32,1024]{2,1,0:T(8,128)S(1)}, u32[]{:S(2)}) %copy-start.2) | copy-done | bytes 8388632
  103.6 2.3 %collective-permute-done.12.refs_0_ = bf16[24,32,1024]{2,1,0:T(8,128)(2,1)} collective-permute-done((bf16[24,32,1024]{2,1,0:T(8,128)(2,1)}, bf16[24,32,1024]{2,1,0:T(8,128)(2,1)}, u32[]{:S(2)}, u32[]{:S(2)}) %collective-permute-start.12) | collective-permute-done | bytes 1572896 | tf_op jit(solution)/shard_map/ppermute | solution.py:250
  105.9 7.2 %collective-permute-start.3 = (bf16[8,32,512]{2,1,0:T(8,128)(2,1)S(1)}, bf16[8,32,512]{2,1,0:T(8,128)(2,1)S(1)}, u32[]{:S(2)}, u32[]{:S(2)}) collective-permute-start(bf16[8,32,512]{2,1,0:T(8,128)(2,1)S(1)} %slice.24), channel_id=1, source_target_pairs={{0,255},{1,2},{2,1},{3,4},{4,3},{5,6},{6,5},{7,8},{8,7},{9,10},{10... | collective-permute-start | bytes 786440 | tf_op jit(solution)/shard_map/ppermute | solution.py:254
  114.4 1.3 collective-permute-start.7
  115.7 3.4 %copy-done.3 = f32[64,32,1024]{2,1,0:T(8,128)S(1)} copy-done((f32[64,32,1024]{2,1,0:T(8,128)S(1)}, f32[64,32,1024]{2,1,0:T(8,128)}, u32[]{:S(2)}) %copy-start.3) | copy-done | bytes 8388632
  119.1 7.3 %shard_map.47.part_ref = f32[64,32,1024]{2,1,0:T(8,128)S(1)} custom-call(bf16[8,5,256,256]{3,2,1,0:T(8,128)(2,1)S(1)} %banded.1.matrix_ref, bf16[64,32,1024]{2,1,0:T(8,128)(2,1)} %collective-permute-done.first_ref, bf16[64,32,1024]{2,1,0:T(8,128)(2,1)} %collective-permute-done.1.second_ref, f32[64,32,1024]{2,1,0:T(8,128)S(1)} %copy-done.3), custom_call_target="tpu_custom_call", output_to_operand_aliasing={{}: (3, {})} | custom-call | flops 2147483648 | bytes 8388608 | tf_op jit(solution)/shard_map/pallas_call | solution.py:137
  126.4 2.9 %shard_map.48.refs_1_ = bf16[64,32,1024]{2,1,0:T(8,128)(2,1)} custom-call(bf16[8,5,256,256]{3,2,1,0:T(8,128)(2,1)S(1)} %banded.1.matrix_ref, f32[64,32,1024]{2,1,0:T(8,128)S(1)} %shard_map.47.part_ref, bf16[32,32,1024]{2,1,0:T(8,128)(2,1)S(1)} %collective-permute-done.13.refs_0_), custom_call_target="tpu_custom_call" | custom-call | flops 536870912 | bytes 4194304 | tf_op jit(solution)/shard_map/pallas_call | solution.py:204
  129.3 3.8 %shard_map.49.refs_5_ = bf16[64,32,1024]{2,1,0:T(8,128)(2,1)} custom-call(bf16[8,5,256,256]{3,2,1,0:T(8,128)(2,1)S(1)} %banded.1.matrix_ref, f32[64,32,1024]{2,1,0:T(8,128)S(1)} %shard_map.47.part_ref, bf16[24,32,1024]{2,1,0:T(8,128)(2,1)} %collective-permute-done.12.refs_0_, bf16[64,32,1024]{2,1,0:T(8,128)(2,1)} %shard_map.48.refs_1_), custom_call_target="tpu_custom_call", output_to_operand_aliasing={{}: (3, {})} | custom-call | flops 402653184 | bytes 3145728 | tf_op jit(solution)/shard_map/pallas_call | solution.py:204
  (41 shorter events, 6.5 us)
Async XLA Ops:
  0.0 66.4 %copy-start.4 = (bf16[64,32,1024]{2,1,0:T(8,128)(2,1)S(1)}, bf16[64,32,1024]{2,1,0:T(8,128)(2,1)}, u32[]{:S(2)}) copy-start(bf16[64,32,1024]{2,1,0:T(8,128)(2,1)} %first_ref.1) | copy-start | bytes 12582916
  0.0 66.4 %copy-start.8 = (bf16[64,64]{1,0:T(8,128)(2,1)S(1)}, bf16[64,64]{1,0:T(8,128)(2,1)}, u32[]{:S(2)}) copy-start(bf16[64,64]{1,0:T(8,128)(2,1)} %weight_ref.1) | copy-start | bytes 24580
  0.0 66.4 %copy-start.9 = (f32[64]{0:T(128)S(1)}, f32[64]{0:T(128)}, u32[]{:S(2)}) copy-start(f32[64]{0:T(128)} %bias_ref.1) | copy-start | bytes 772
  0.0 55.2 %collective-permute-start = (bf16[64,32,1024]{2,1,0:T(8,128)(2,1)}, bf16[64,32,1024]{2,1,0:T(8,128)(2,1)}, u32[]{:S(2)}, u32[]{:S(2)}) collective-permute-start(bf16[64,32,1024]{2,1,0:T(8,128)(2,1)} %first_ref.1), channel_id=1, source_target_pairs={{0,254},{1,3},{2,0},{3,5},{4,2},{5,7},{6,4},{7,9},{8,6},{9,11},{10... | collective-permute-start | bytes 12582920 | tf_op jit(solution)/shard_map/ppermute | solution.py:244
  8.9 46.3 %collective-permute-start.2 = (bf16[64,32,1024]{2,1,0:T(8,128)(2,1)}, bf16[64,32,1024]{2,1,0:T(8,128)(2,1)S(1)}, u32[]{:S(2)}, u32[]{:S(2)}) collective-permute-start(bf16[64,32,1024]{2,1,0:T(8,128)(2,1)} %first_ref.1), channel_id=1, source_target_pairs={{0,1},{1,0},{2,3},{3,2},{4,5},{5,4},{6,7},{7,6},{8,9},{9,8},{10,11... | collective-permute-start | bytes 12582920 | tf_op jit(solution)/shard_map/ppermute | solution.py:245
  55.2 59.2 %collective-permute-start.1 = (bf16[64,32,1024]{2,1,0:T(8,128)(2,1)}, bf16[64,32,1024]{2,1,0:T(8,128)(2,1)}, u32[]{:S(2)}, u32[]{:S(2)}) collective-permute-start(bf16[64,32,1024]{2,1,0:T(8,128)(2,1)} %collective-permute-done.first_ref), channel_id=1, source_target_pairs={{0,1},{1,0},{2,3},{3,2},{4,5},{5,4},{6,7},{7,6},{8,9},{9,8},{10,11... | collective-permute-start | bytes 12582920 | tf_op jit(solution)/shard_map/ppermute | solution.py:264
  55.2 16.2 %copy-start.6 = (bf16[64,32,1024]{2,1,0:T(8,128)(2,1)}, bf16[64,32,1024]{2,1,0:T(8,128)(2,1)S(1)}, u32[]{:S(2)}) copy-start(bf16[64,32,1024]{2,1,0:T(8,128)(2,1)S(1)} %collective-permute-done.2.second_ref) | copy-start | bytes 12582916
  57.0 56.1 %collective-permute-start.13 = (bf16[32,32,1024]{2,1,0:T(8,128)(2,1)}, bf16[32,32,1024]{2,1,0:T(8,128)(2,1)S(1)}, u32[]{:S(2)}, u32[]{:S(2)}) collective-permute-start(bf16[32,32,1024]{2,1,0:T(8,128)(2,1)} %slice.28), channel_id=1, source_target_pairs={{0,255},{1,2},{2,1},{3,4},{4,3},{5,6},{6,5},{7,8},{8,7},{9,10},{10... | collective-permute-start | bytes 6291464 | tf_op jit(solution)/shard_map/ppermute | solution.py:250
  66.3 11.0 %copy-start.10 = (bf16[8,8,8,129]{3,2,1,0:T(8,128)(2,1)S(1)}, bf16[8,8,8,129]{3,2,1,0:T(8,128)(2,1)}, u32[]{:S(2)}) copy-start(bf16[8,8,8,129]{3,2,1,0:T(8,128)(2,1)} %param.5) | copy-start | bytes 396292
  66.3 39.6 %collective-permute-start.12 = (bf16[24,32,1024]{2,1,0:T(8,128)(2,1)}, bf16[24,32,1024]{2,1,0:T(8,128)(2,1)}, u32[]{:S(2)}, u32[]{:S(2)}) collective-permute-start(bf16[24,32,1024]{2,1,0:T(8,128)(2,1)} %slice.27), channel_id=1, source_target_pairs={{0,255},{1,2},{2,1},{3,4},{4,3},{5,6},{6,5},{7,8},{8,7},{9,10},{10... | collective-permute-start | bytes 4718600 | tf_op jit(solution)/shard_map/ppermute | solution.py:250
  71.4 3.3 %copy-start = (f32[64,32,1024]{2,1,0:T(8,128)}, f32[64,32,1024]{2,1,0:T(8,128)S(1)}, u32[]{:S(2)}) copy-start(f32[64,32,1024]{2,1,0:T(8,128)S(1)} %mix.1.part_ref) | copy-start | bytes 25165828
  74.7 13.8 %collective-permute-start.9 = (bf16[8,32,256]{2,1,0:T(8,128)(2,1)S(1)}, bf16[8,32,256]{2,1,0:T(8,128)(2,1)S(1)}, u32[]{:S(2)}, u32[]{:S(2)}) collective-permute-start(bf16[8,32,256]{2,1,0:T(8,128)(2,1)S(1)} %get-tuple-element.5), channel_id=1, source_target_pairs={{255,247},{0,17},{63,55},{64,81},{127,119},{128,145},{191,183},{19... | collective-permute-start | bytes 393224 | tf_op jit(solution)/shard_map/ppermute | solution.py:262
  76.0 13.2 %collective-permute-start.5 = (bf16[8,32,256]{2,1,0:T(8,128)(2,1)S(1)}, bf16[8,32,256]{2,1,0:T(8,128)(2,1)S(1)}, u32[]{:S(2)}, u32[]{:S(2)}) collective-permute-start(bf16[8,32,256]{2,1,0:T(8,128)(2,1)S(1)} %get-tuple-element.6), channel_id=1, source_target_pairs={{255,239},{0,9},{63,47},{64,73},{127,111},{128,137},{191,175},{192... | collective-permute-start | bytes 393224 | tf_op jit(solution)/shard_map/ppermute | solution.py:262
  84.1 5.7 %copy-start.5 = (bf16[64,32,1024]{2,1,0:T(8,128)(2,1)S(1)}, bf16[64,32,1024]{2,1,0:T(8,128)(2,1)}, u32[]{:S(2)}) copy-start(bf16[64,32,1024]{2,1,0:T(8,128)(2,1)} %first_ref.1) | copy-start | bytes 12582916
  88.5 13.8 %collective-permute-start.10 = (bf16[8,32,256]{2,1,0:T(8,128)(2,1)S(1)}, bf16[8,32,256]{2,1,0:T(8,128)(2,1)S(1)}, u32[]{:S(2)}, u32[]{:S(2)}) collective-permute-start(bf16[8,32,256]{2,1,0:T(8,128)(2,1)S(1)} %collective-permute-done.9), channel_id=1, source_target_pairs={{247,49},{17,215},{55,113},{81,23},{119,177},{145,87},{183,241},{2... | collective-permute-start | bytes 393224 | tf_op jit(solution)/shard_map/ppermute | solution.py:262
  89.2 13.8 %collective-permute-start.6 = (bf16[8,32,256]{2,1,0:T(8,128)(2,1)S(1)}, bf16[8,32,256]{2,1,0:T(8,128)(2,1)S(1)}, u32[]{:S(2)}, u32[]{:S(2)}) collective-permute-start(bf16[8,32,256]{2,1,0:T(8,128)(2,1)S(1)} %collective-permute-done.5), channel_id=1, source_target_pairs={{239,41},{9,207},{47,105},{73,15},{111,169},{137,79},{175,233},{20... | collective-permute-start | bytes 393224 | tf_op jit(solution)/shard_map/ppermute | solution.py:262
  89.8 3.4 %copy-start.1 = (f32[64,32,1024]{2,1,0:T(8,128)S(1)}, f32[64,32,1024]{2,1,0:T(8,128)}, u32[]{:S(2)}) copy-start(f32[64,32,1024]{2,1,0:T(8,128)} %copy-done) | copy-start | bytes 25165828
  99.0 3.3 %copy-start.2 = (f32[64,32,1024]{2,1,0:T(8,128)}, f32[64,32,1024]{2,1,0:T(8,128)S(1)}, u32[]{:S(2)}) copy-start(f32[64,32,1024]{2,1,0:T(8,128)S(1)} %shard_map.46.part_ref) | copy-start | bytes 25165828
  102.3 30.9 %collective-permute-start.4 = (bf16[8,32,256]{2,1,0:T(8,128)(2,1)S(1)}, bf16[8,32,256]{2,1,0:T(8,128)(2,1)S(1)}, u32[]{:S(2)}, u32[]{:S(2)}) collective-permute-start(bf16[8,32,256]{2,1,0:T(8,128)(2,1)S(1)} %get-tuple-element.6), channel_id=1, source_target_pairs={{1,2},{2,1},{3,4},{4,3},{5,6},{6,5},{7,8},{8,7},{9,10},{10,9},{11,... | collective-permute-start | bytes 393224 | tf_op jit(solution)/shard_map/ppermute | solution.py:260
  102.9 30.2 %collective-permute-start.8 = (bf16[8,32,256]{2,1,0:T(8,128)(2,1)S(1)}, bf16[8,32,256]{2,1,0:T(8,128)(2,1)S(1)}, u32[]{:S(2)}, u32[]{:S(2)}) collective-permute-start(bf16[8,32,256]{2,1,0:T(8,128)(2,1)S(1)} %get-tuple-element.5), channel_id=1, source_target_pairs={{1,2},{2,1},{3,4},{4,3},{5,6},{6,5},{7,8},{8,7},{9,10},{10,9},{11,... | collective-permute-start | bytes 393224 | tf_op jit(solution)/shard_map/ppermute | solution.py:260
  105.9 27.2 %collective-permute-start.3 = (bf16[8,32,512]{2,1,0:T(8,128)(2,1)S(1)}, bf16[8,32,512]{2,1,0:T(8,128)(2,1)S(1)}, u32[]{:S(2)}, u32[]{:S(2)}) collective-permute-start(bf16[8,32,512]{2,1,0:T(8,128)(2,1)S(1)} %slice.24), channel_id=1, source_target_pairs={{0,255},{1,2},{2,1},{3,4},{4,3},{5,6},{6,5},{7,8},{8,7},{9,10},{10... | collective-permute-start | bytes 786440 | tf_op jit(solution)/shard_map/ppermute | solution.py:254
  113.1 20.1 %collective-permute-start.11 = (bf16[8,32,256]{2,1,0:T(8,128)(2,1)S(1)}, bf16[8,32,256]{2,1,0:T(8,128)(2,1)S(1)}, u32[]{:S(2)}, u32[]{:S(2)}) collective-permute-start(bf16[8,32,256]{2,1,0:T(8,128)(2,1)S(1)} %collective-permute-done.10), channel_id=1, source_target_pairs={{49,0},{215,255},{113,64},{23,63},{177,128},{87,127},{241,192},{15... | collective-permute-start | bytes 393224 | tf_op jit(solution)/shard_map/ppermute | solution.py:262
  114.4 18.8 %collective-permute-start.7 = (bf16[8,32,256]{2,1,0:T(8,128)(2,1)S(1)}, bf16[8,32,256]{2,1,0:T(8,128)(2,1)S(1)}, u32[]{:S(2)}, u32[]{:S(2)}) collective-permute-start(bf16[8,32,256]{2,1,0:T(8,128)(2,1)S(1)} %collective-permute-done.6), channel_id=1, source_target_pairs={{41,0},{207,255},{105,64},{15,63},{169,128},{79,127},{233,192},{14... | collective-permute-start | bytes 393224 | tf_op jit(solution)/shard_map/ppermute | solution.py:262
  115.7 3.4 %copy-start.3 = (f32[64,32,1024]{2,1,0:T(8,128)S(1)}, f32[64,32,1024]{2,1,0:T(8,128)}, u32[]{:S(2)}) copy-start(f32[64,32,1024]{2,1,0:T(8,128)} %copy-done.2) | copy-start | bytes 25165828
  (1 other events, 2.2 us)

commit v5 on v4

--- a/solution.py
+++ b/solution.py
@@ -8,8 +8,8 @@
 from jax.sharding import PartitionSpec as P
 
 FAR, RING_TWIN, OWN, TWIN, RING = range(5)
-FAR_CHUNKS = (4, 3)
-RELAY_PLANES = ((5, 1), (6, 2))
+FAR_CHUNKS = (5, 2)
+RELAYS = ((5, 1, False), (6, 2, True))
 WHOLE = pl.BlockSpec(memory_space=pltpu.VMEM)
 GRANT = pltpu.CompilerParams(vmem_limit_bytes=16 * 2**20)
 
@@ -218,7 +218,7 @@
     )(matrices, part, *fars, *given)
 
 
-def relay_hops(devices, up_plane, down_plane):
+def relay_hops(devices, up_plane, down_plane, inner):
     if devices != 256:
         return [], [], []
 
@@ -230,6 +230,10 @@
         low, high = strip(x - 1, 7, 3, 1), strip(x, 0, 0, 0)
         paths.append([low, strip(x - 1, up_plane, 3, 1), strip(x, up_plane, 0, 1), high])
         paths.append([high, strip(x, down_plane, 0, 1), strip(x - 1, down_plane, 3, 1), low])
+        for z in range(1, 8) if inner else ():
+            low, high = strip(x, z - 1, 3, 1), strip(x, z, 0, 0)
+            paths.append([low, strip(x, z - 1, 2, 1), strip(x, z - 1, 1, 1), high])
+            paths.append([high, strip(x, z, 1, 0), strip(x, z, 2, 0), low])
     return tuple([tuple(path[i : i + 2]) for path in paths] for i in range(3))
 
 
@@ -250,11 +254,11 @@
         fars.append(lax.ppermute(piece, "strip", far_route))
         start += count
     end = twin[start * width :]
-    cuts = [0, columns // 2, 3 * columns // 4, columns]
+    cuts = [0, 3 * columns // 8, 3 * columns // 4, columns]
     ends = [lax.ppermute(end[:, :, : cuts[1]], "strip", far_route)]
-    for t, planes in enumerate(RELAY_PLANES, 1):
+    for t, relay in enumerate(RELAYS, 1):
         piece = end[:, :, cuts[t] : cuts[t + 1]]
-        hops = relay_hops(devices, *planes)
+        hops = relay_hops(devices, *relay)
         relayed = [target for _, target in hops[2]]
         route = [pair for pair in far_route if pair[1] not in relayed]
         ends.append(lax.ppermute(piece, "strip", route))

time: 136 us -> 136 us (level)
  no operation moved by 1% of the time
where the time goes in v5:
time: 136 us; the launch traced here: 135 us
  waiting for transfers between devices  47.8 us (35%)
  starting transfers between devices  33.3 us (24%)
  Pallas kernels  27 us (20%)
  local copies, waits for them, and re-layouts  26 us (19%)
    ppermute x1, waiting for transfers between devices, local(): ring = lax.ppermute(features, 'strip', ring_route)  46.3 us
    unnamed x22, local copies, waits for them, and re-layouts  15.5 us
    pallas_call x2, Pallas kernels, add_pair(): pl.pallas_call(functools.partial(pair_kernel, first_role, second_role), g...  10.8 us
    ppermute x1, starting transfers between devices, local(): ring = lax.ppermute(features, 'strip', ring_route)  8.87 us
    ppermute x2, starting transfers between devices, local(): fars.append(lax.ppermute(piece, 'strip', far_route))  8.08 us
    pallas_call x3, Pallas kernels, finish(): pl.pallas_call(functools.partial(last_kernel, start, count, cuts), in_spe...  7.86 us
    ppermute x6, starting transfers between devices, local(): piece = lax.ppermute(piece, 'strip', hop)  7.84 us
    ppermute x1, starting transfers between devices, local(): ends = [lax.ppermute(end[:, :, :cuts[1]], 'strip', far_route)]  7.17 us
  transfers between devices with their start and end apart: 14, of which 2 were waited for; matrix products, arithmetic and copies ran while one was open for 8% of the time, Pallas kernels for 19%

profile of v5, /device:TPU:0, one launch (start us, length us, event | category | flops | bytes accessed | tf_op | source)
XLA Modules:
  0.0 134.5 jit_solution(1981795190505168882)
XLA Ops:
  0.0 8.9 %collective-permute-start = (bf16[64,32,1024]{2,1,0:T(8,128)(2,1)}, bf16[64,32,1024]{2,1,0:T(8,128)(2,1)}, u32[]{:S(2)}, u32[]{:S(2)}) collective-permute-start(bf16[64,32,1024]{2,1,0:T(8,128)(2,1)} %first_ref.1), channel_id=1, source_target_pairs={{0,254},{1,3},{2,0},{3,5},{4,2},{5,7},{6,4},{7,9},{8,6},{9,11},{10... | collective-permute-start | bytes 12582920 | tf_op jit(solution)/shard_map/ppermute | solution.py:248
  8.9 46.3 %collective-permute-done.first_ref = bf16[64,32,1024]{2,1,0:T(8,128)(2,1)} collective-permute-done((bf16[64,32,1024]{2,1,0:T(8,128)(2,1)}, bf16[64,32,1024]{2,1,0:T(8,128)(2,1)}, u32[]{:S(2)}, u32[]{:S(2)}) %collective-permute-start) | collective-permute-done | bytes 4194336 | tf_op jit(solution)/shard_map/ppermute | solution.py:248
  55.2 2.0 %slice.28 = bf16[40,32,1024]{2,1,0:T(8,128)(2,1)} slice(bf16[64,32,1024]{2,1,0:T(8,128)(2,1)S(1)} %collective-permute-done.2.second_ref), slice={[0:40], [0:32], [0:1024]} | slice | bytes 5242880 | tf_op jit(solution)/shard_map/slice | solution.py:253
  57.2 8.0 %collective-permute-start.13 = (bf16[40,32,1024]{2,1,0:T(8,128)(2,1)}, bf16[40,32,1024]{2,1,0:T(8,128)(2,1)S(1)}, u32[]{:S(2)}, u32[]{:S(2)}) collective-permute-start(bf16[40,32,1024]{2,1,0:T(8,128)(2,1)} %slice.28), channel_id=1, source_target_pairs={{0,255},{1,2},{2,1},{3,4},{4,3},{5,6},{6,5},{7,8},{8,7},{9,10},{10... | collective-permute-start | bytes 7864328 | tf_op jit(solution)/shard_map/ppermute | solution.py:254
  66.5 4.9 %mix.1.part_ref = f32[64,32,1024]{2,1,0:T(8,128)S(1)} custom-call(f32[64]{0:T(128)S(1)} %copy-done.9, bf16[64,64]{1,0:T(8,128)(2,1)S(1)} %copy-done.8, bf16[64,32,1024]{2,1,0:T(8,128)(2,1)S(1)} %copy-done.4), custom_call_target="tpu_custom_call" | custom-call | flops 2147483648 | bytes 12582912 | tf_op jit(solution)/shard_map/mix/pallas_call | solution.py:97
  71.5 3.3 %copy-done = f32[64,32,1024]{2,1,0:T(8,128)} copy-done((f32[64,32,1024]{2,1,0:T(8,128)}, f32[64,32,1024]{2,1,0:T(8,128)S(1)}, u32[]{:S(2)}) %copy-start) | copy-done | bytes 8388632
  74.8 2.0 %collective-permute-start.5 = (bf16[8,32,384]{2,1,0:T(8,128)(2,1)S(1)}, bf16[8,32,384]{2,1,0:T(8,128)(2,1)}, u32[]{:S(2)}, u32[]{:S(2)}) collective-permute-start(bf16[8,32,384]{2,1,0:T(8,128)(2,1)S(1)} %get-tuple-element.5), channel_id=1, source_target_pairs={{255,239},{0,9},{63,47},{64,73},{127,111},{128,137},{191,175},{192... | collective-permute-start | bytes 589832 | tf_op jit(solution)/shard_map/ppermute | solution.py:266
  77.4 1.9 %collective-permute-start.9 = (bf16[8,32,256]{2,1,0:T(8,128)(2,1)}, bf16[8,32,256]{2,1,0:T(8,128)(2,1)}, u32[]{:S(2)}, u32[]{:S(2)}) collective-permute-start(bf16[8,32,256]{2,1,0:T(8,128)(2,1)} %slice.26), channel_id=1, source_target_pairs={{255,247},{0,17},{7,5},{8,10},{15,13},{16,18},{23,21},{24,26},{31,... | collective-permute-start | bytes 393224 | tf_op jit(solution)/shard_map/ppermute | solution.py:266
  79.5 1.8 %reshape.20 = f32[8,8,8,6,32]{4,3,2,1,0:T(8,128)} reshape(f32[8,8,8,192]{3,2,1,0:T(8,128)S(1)} %pad_convert_fusion) | data formatting | bytes 786432 | tf_op jit(solution)/shard_map/reshape | solution.py:48
  81.3 3.1 %copy.10 = f32[8,6,8,8,32]{4,3,2,1,0:T(8,128)} copy(f32[8,6,8,8,32]{4,1,3,2,0:T(8,128)} %bitcast.6) | data formatting | bytes 786432 | tf_op jit(solution)/shard_map/reshape | solution.py:48
  84.3 1.9 %reshape.17.rows_ref = f32[8,6,8,256]{3,2,1,0:T(8,128)S(1)} reshape(f32[8,6,8,8,32]{4,3,2,1,0:T(8,128)} %copy.10) | data formatting | bytes 786432 | tf_op jit(solution)/shard_map/reshape | solution.py:48
  86.2 3.4 %banded.1.matrix_ref = bf16[8,5,256,256]{3,2,1,0:T(8,128)(2,1)S(1)} custom-call(s32[1]{0:T(128)} %bitcast.odd_ref, f32[8,6,8,256]{3,2,1,0:T(8,128)S(1)} %reshape.17.rows_ref), custom_call_target="tpu_custom_call" | custom-call | flops 1000000000 | bytes 4000000 | tf_op jit(solution)/shard_map/banded/pallas_call | solution.py:49
  91.0 3.4 %copy-done.1 = f32[64,32,1024]{2,1,0:T(8,128)S(1)} copy-done((f32[64,32,1024]{2,1,0:T(8,128)S(1)}, f32[64,32,1024]{2,1,0:T(8,128)}, u32[]{:S(2)}) %copy-start.1) | copy-done | bytes 8388632
  94.3 2.2 %copy-done.7 = bf16[64,32,1024]{2,1,0:T(8,128)(2,1)S(1)} copy-done((bf16[64,32,1024]{2,1,0:T(8,128)(2,1)S(1)}, bf16[64,32,1024]{2,1,0:T(8,128)(2,1)}, u32[]{:S(2)}) %copy-start.7) | copy-done | bytes 4194328
  96.5 3.6 %shard_map.46.part_ref = f32[64,32,1024]{2,1,0:T(8,128)S(1)} custom-call(bf16[8,5,256,256]{3,2,1,0:T(8,128)(2,1)S(1)} %banded.1.matrix_ref, bf16[64,32,1024]{2,1,0:T(8,128)(2,1)S(1)} %copy-done.5, bf16[64,32,1024]{2,1,0:T(8,128)(2,1)S(1)} %copy-done.7, f32[64,32,1024]{2,1,0:T(8,128)S(1)} %copy-done.1), custom_call_target="tpu_custom_call", output_to_operand_aliasing={{}: (3, {})} | custom-call | flops 2147483648 | bytes 8388608 | tf_op jit(solution)/shard_map/pallas_call | solution.py:137
  100.1 3.3 %copy-done.2 = f32[64,32,1024]{2,1,0:T(8,128)} copy-done((f32[64,32,1024]{2,1,0:T(8,128)}, f32[64,32,1024]{2,1,0:T(8,128)S(1)}, u32[]{:S(2)}) %copy-start.2) | copy-done | bytes 8388632
  104.7 1.4 %collective-permute-done.12.refs_0_ = bf16[16,32,1024]{2,1,0:T(8,128)(2,1)} collective-permute-done((bf16[16,32,1024]{2,1,0:T(8,128)(2,1)}, bf16[16,32,1024]{2,1,0:T(8,128)(2,1)}, u32[]{:S(2)}, u32[]{:S(2)}) %collective-permute-start.12) | collective-permute-done | bytes 1048608 | tf_op jit(solution)/shard_map/ppermute | solution.py:254
  106.1 7.2 %collective-permute-start.3 = (bf16[8,32,384]{2,1,0:T(8,128)(2,1)S(1)}, bf16[8,32,384]{2,1,0:T(8,128)(2,1)S(1)}, u32[]{:S(2)}, u32[]{:S(2)}) collective-permute-start(bf16[8,32,384]{2,1,0:T(8,128)(2,1)S(1)} %get-tuple-element.6), channel_id=1, source_target_pairs={{0,255},{1,2},{2,1},{3,4},{4,3},{5,6},{6,5},{7,8},{8,7},{9,10},{10... | collective-permute-start | bytes 589832 | tf_op jit(solution)/shard_map/ppermute | solution.py:258
  114.6 1.3 collective-permute-start.7
  115.9 3.4 %copy-done.3 = f32[64,32,1024]{2,1,0:T(8,128)S(1)} copy-done((f32[64,32,1024]{2,1,0:T(8,128)S(1)}, f32[64,32,1024]{2,1,0:T(8,128)}, u32[]{:S(2)}) %copy-start.3) | copy-done | bytes 8388632
  119.3 7.3 %shard_map.47.part_ref = f32[64,32,1024]{2,1,0:T(8,128)S(1)} custom-call(bf16[8,5,256,256]{3,2,1,0:T(8,128)(2,1)S(1)} %banded.1.matrix_ref, bf16[64,32,1024]{2,1,0:T(8,128)(2,1)} %collective-permute-done.first_ref, bf16[64,32,1024]{2,1,0:T(8,128)(2,1)} %collective-permute-done.1.second_ref, f32[64,32,1024]{2,1,0:T(8,128)S(1)} %copy-done.3), custom_call_target="tpu_custom_call", output_to_operand_aliasing={{}: (3, {})} | custom-call | flops 2147483648 | bytes 8388608 | tf_op jit(solution)/shard_map/pallas_call | solution.py:137
  126.6 3.5 %shard_map.48.refs_1_ = bf16[64,32,1024]{2,1,0:T(8,128)(2,1)} custom-call(bf16[8,5,256,256]{3,2,1,0:T(8,128)(2,1)S(1)} %banded.1.matrix_ref, f32[64,32,1024]{2,1,0:T(8,128)S(1)} %shard_map.47.part_ref, bf16[40,32,1024]{2,1,0:T(8,128)(2,1)S(1)} %collective-permute-done.13.refs_0_), custom_call_target="tpu_custom_call" | custom-call | flops 671088640 | bytes 5242880 | tf_op jit(solution)/shard_map/pallas_call | solution.py:204
  130.1 3.0 %shard_map.49.refs_5_ = bf16[64,32,1024]{2,1,0:T(8,128)(2,1)} custom-call(bf16[8,5,256,256]{3,2,1,0:T(8,128)(2,1)S(1)} %banded.1.matrix_ref, f32[64,32,1024]{2,1,0:T(8,128)S(1)} %shard_map.47.part_ref, bf16[16,32,1024]{2,1,0:T(8,128)(2,1)} %collective-permute-done.12.refs_0_, bf16[64,32,1024]{2,1,0:T(8,128)(2,1)} %shard_map.48.refs_1_), custom_call_target="tpu_custom_call", output_to_operand_aliasing={{}: (3, {})} | custom-call | flops 268435456 | bytes 2097152 | tf_op jit(solution)/shard_map/pallas_call | solution.py:204
  133.2 1.3 shard_map.50
  (41 shorter events, 6.1 us)
Async XLA Ops:
  0.0 66.5 %copy-start.4 = (bf16[64,32,1024]{2,1,0:T(8,128)(2,1)S(1)}, bf16[64,32,1024]{2,1,0:T(8,128)(2,1)}, u32[]{:S(2)}) copy-start(bf16[64,32,1024]{2,1,0:T(8,128)(2,1)} %first_ref.1) | copy-start | bytes 12582916
  0.0 66.5 %copy-start.8 = (bf16[64,64]{1,0:T(8,128)(2,1)S(1)}, bf16[64,64]{1,0:T(8,128)(2,1)}, u32[]{:S(2)}) copy-start(bf16[64,64]{1,0:T(8,128)(2,1)} %weight_ref.1) | copy-start | bytes 24580
  0.0 66.5 %copy-start.9 = (f32[64]{0:T(128)S(1)}, f32[64]{0:T(128)}, u32[]{:S(2)}) copy-start(f32[64]{0:T(128)} %bias_ref.1) | copy-start | bytes 772
  0.0 55.2 %collective-permute-start = (bf16[64,32,1024]{2,1,0:T(8,128)(2,1)}, bf16[64,32,1024]{2,1,0:T(8,128)(2,1)}, u32[]{:S(2)}, u32[]{:S(2)}) collective-permute-start(bf16[64,32,1024]{2,1,0:T(8,128)(2,1)} %first_ref.1), channel_id=1, source_target_pairs={{0,254},{1,3},{2,0},{3,5},{4,2},{5,7},{6,4},{7,9},{8,6},{9,11},{10... | collective-permute-start | bytes 12582920 | tf_op jit(solution)/shard_map/ppermute | solution.py:248
  8.9 46.3 %collective-permute-start.2 = (bf16[64,32,1024]{2,1,0:T(8,128)(2,1)}, bf16[64,32,1024]{2,1,0:T(8,128)(2,1)S(1)}, u32[]{:S(2)}, u32[]{:S(2)}) collective-permute-start(bf16[64,32,1024]{2,1,0:T(8,128)(2,1)} %first_ref.1), channel_id=1, source_target_pairs={{0,1},{1,0},{2,3},{3,2},{4,5},{5,4},{6,7},{7,6},{8,9},{9,8},{10,11... | collective-permute-start | bytes 12582920 | tf_op jit(solution)/shard_map/ppermute | solution.py:249
  55.2 59.4 %collective-permute-start.1 = (bf16[64,32,1024]{2,1,0:T(8,128)(2,1)}, bf16[64,32,1024]{2,1,0:T(8,128)(2,1)}, u32[]{:S(2)}, u32[]{:S(2)}) collective-permute-start(bf16[64,32,1024]{2,1,0:T(8,128)(2,1)} %collective-permute-done.first_ref), channel_id=1, source_target_pairs={{0,1},{1,0},{2,3},{3,2},{4,5},{5,4},{6,7},{7,6},{8,9},{9,8},{10,11... | collective-permute-start | bytes 12582920 | tf_op jit(solution)/shard_map/ppermute | solution.py:268
  55.2 21.5 %copy-start.6 = (bf16[64,32,1024]{2,1,0:T(8,128)(2,1)}, bf16[64,32,1024]{2,1,0:T(8,128)(2,1)S(1)}, u32[]{:S(2)}) copy-start(bf16[64,32,1024]{2,1,0:T(8,128)(2,1)S(1)} %collective-permute-done.2.second_ref) | copy-start | bytes 12582916
  57.2 56.1 %collective-permute-start.13 = (bf16[40,32,1024]{2,1,0:T(8,128)(2,1)}, bf16[40,32,1024]{2,1,0:T(8,128)(2,1)S(1)}, u32[]{:S(2)}, u32[]{:S(2)}) collective-permute-start(bf16[40,32,1024]{2,1,0:T(8,128)(2,1)} %slice.28), channel_id=1, source_target_pairs={{0,255},{1,2},{2,1},{3,4},{4,3},{5,6},{6,5},{7,8},{8,7},{9,10},{10... | collective-permute-start | bytes 7864328 | tf_op jit(solution)/shard_map/ppermute | solution.py:254
  66.4 12.9 %copy-start.10 = (bf16[8,8,8,129]{3,2,1,0:T(8,128)(2,1)S(1)}, bf16[8,8,8,129]{3,2,1,0:T(8,128)(2,1)}, u32[]{:S(2)}) copy-start(bf16[8,8,8,129]{3,2,1,0:T(8,128)(2,1)} %param.5) | copy-start | bytes 396292
  66.4 39.7 %collective-permute-start.12 = (bf16[16,32,1024]{2,1,0:T(8,128)(2,1)}, bf16[16,32,1024]{2,1,0:T(8,128)(2,1)}, u32[]{:S(2)}, u32[]{:S(2)}) collective-permute-start(bf16[16,32,1024]{2,1,0:T(8,128)(2,1)} %slice.27), channel_id=1, source_target_pairs={{0,255},{1,2},{2,1},{3,4},{4,3},{5,6},{6,5},{7,8},{8,7},{9,10},{10... | collective-permute-start | bytes 3145736 | tf_op jit(solution)/shard_map/ppermute | solution.py:254
  71.5 3.3 %copy-start = (f32[64,32,1024]{2,1,0:T(8,128)}, f32[64,32,1024]{2,1,0:T(8,128)S(1)}, u32[]{:S(2)}) copy-start(f32[64,32,1024]{2,1,0:T(8,128)S(1)} %mix.1.part_ref) | copy-start | bytes 25165828
  74.8 15.5 %collective-permute-start.5 = (bf16[8,32,384]{2,1,0:T(8,128)(2,1)S(1)}, bf16[8,32,384]{2,1,0:T(8,128)(2,1)}, u32[]{:S(2)}, u32[]{:S(2)}) collective-permute-start(bf16[8,32,384]{2,1,0:T(8,128)(2,1)S(1)} %get-tuple-element.5), channel_id=1, source_target_pairs={{255,239},{0,9},{63,47},{64,73},{127,111},{128,137},{191,175},{192... | collective-permute-start | bytes 589832 | tf_op jit(solution)/shard_map/ppermute | solution.py:266
  77.4 12.2 %collective-permute-start.9 = (bf16[8,32,256]{2,1,0:T(8,128)(2,1)}, bf16[8,32,256]{2,1,0:T(8,128)(2,1)}, u32[]{:S(2)}, u32[]{:S(2)}) collective-permute-start(bf16[8,32,256]{2,1,0:T(8,128)(2,1)} %slice.26), channel_id=1, source_target_pairs={{255,247},{0,17},{7,5},{8,10},{15,13},{16,18},{23,21},{24,26},{31,... | collective-permute-start | bytes 393224 | tf_op jit(solution)/shard_map/ppermute | solution.py:266
  86.2 4.8 %copy-start.5 = (bf16[64,32,1024]{2,1,0:T(8,128)(2,1)S(1)}, bf16[64,32,1024]{2,1,0:T(8,128)(2,1)}, u32[]{:S(2)}) copy-start(bf16[64,32,1024]{2,1,0:T(8,128)(2,1)} %first_ref.1) | copy-start | bytes 12582916
  89.6 13.8 %collective-permute-start.10 = (bf16[8,32,256]{2,1,0:T(8,128)(2,1)}, bf16[8,32,256]{2,1,0:T(8,128)(2,1)S(1)}, u32[]{:S(2)}, u32[]{:S(2)}) collective-permute-start(bf16[8,32,256]{2,1,0:T(8,128)(2,1)} %collective-permute-done.9), channel_id=1, source_target_pairs={{247,49},{17,215},{5,3},{10,12},{13,11},{18,20},{21,19},{26,28},{2... | collective-permute-start | bytes 393224 | tf_op jit(solution)/shard_map/ppermute | solution.py:266
  90.3 13.8 %collective-permute-start.6 = (bf16[8,32,384]{2,1,0:T(8,128)(2,1)}, bf16[8,32,384]{2,1,0:T(8,128)(2,1)S(1)}, u32[]{:S(2)}, u32[]{:S(2)}) collective-permute-start(bf16[8,32,384]{2,1,0:T(8,128)(2,1)} %collective-permute-done.5), channel_id=1, source_target_pairs={{239,41},{9,207},{47,105},{73,15},{111,169},{137,79},{175,233},{20... | collective-permute-start | bytes 589832 | tf_op jit(solution)/shard_map/ppermute | solution.py:266
  91.0 3.4 %copy-start.1 = (f32[64,32,1024]{2,1,0:T(8,128)S(1)}, f32[64,32,1024]{2,1,0:T(8,128)}, u32[]{:S(2)}) copy-start(f32[64,32,1024]{2,1,0:T(8,128)} %copy-done) | copy-start | bytes 25165828
  100.1 3.3 %copy-start.2 = (f32[64,32,1024]{2,1,0:T(8,128)}, f32[64,32,1024]{2,1,0:T(8,128)S(1)}, u32[]{:S(2)}) copy-start(f32[64,32,1024]{2,1,0:T(8,128)S(1)} %shard_map.46.part_ref) | copy-start | bytes 25165828
  103.4 29.8 %collective-permute-start.4 = (bf16[8,32,384]{2,1,0:T(8,128)(2,1)S(1)}, bf16[8,32,384]{2,1,0:T(8,128)(2,1)S(1)}, u32[]{:S(2)}, u32[]{:S(2)}) collective-permute-start(bf16[8,32,384]{2,1,0:T(8,128)(2,1)S(1)} %get-tuple-element.5), channel_id=1, source_target_pairs={{1,2},{2,1},{3,4},{4,3},{5,6},{6,5},{7,8},{8,7},{9,10},{10,9},{11,... | collective-permute-start | bytes 589832 | tf_op jit(solution)/shard_map/ppermute | solution.py:264
  104.1 29.1 %collective-permute-start.8 = (bf16[8,32,256]{2,1,0:T(8,128)(2,1)}, bf16[8,32,256]{2,1,0:T(8,128)(2,1)S(1)}, u32[]{:S(2)}, u32[]{:S(2)}) collective-permute-start(bf16[8,32,256]{2,1,0:T(8,128)(2,1)} %slice.26), channel_id=1, source_target_pairs={{1,2},{2,1},{3,4},{4,3},{5,6},{6,5},{9,10},{10,9},{11,12},{12,11},... | collective-permute-start | bytes 393224 | tf_op jit(solution)/shard_map/ppermute | solution.py:264
  106.1 27.0 %collective-permute-start.3 = (bf16[8,32,384]{2,1,0:T(8,128)(2,1)S(1)}, bf16[8,32,384]{2,1,0:T(8,128)(2,1)S(1)}, u32[]{:S(2)}, u32[]{:S(2)}) collective-permute-start(bf16[8,32,384]{2,1,0:T(8,128)(2,1)S(1)} %get-tuple-element.6), channel_id=1, source_target_pairs={{0,255},{1,2},{2,1},{3,4},{4,3},{5,6},{6,5},{7,8},{8,7},{9,10},{10... | collective-permute-start | bytes 589832 | tf_op jit(solution)/shard_map/ppermute | solution.py:258
  113.3 19.9 %collective-permute-start.11 = (bf16[8,32,256]{2,1,0:T(8,128)(2,1)S(1)}, bf16[8,32,256]{2,1,0:T(8,128)(2,1)S(1)}, u32[]{:S(2)}, u32[]{:S(2)}) collective-permute-start(bf16[8,32,256]{2,1,0:T(8,128)(2,1)S(1)} %collective-permute-done.10), channel_id=1, source_target_pairs={{49,0},{215,255},{3,8},{12,7},{11,16},{20,15},{19,24},{28,23},{27,... | collective-permute-start | bytes 393224 | tf_op jit(solution)/shard_map/ppermute | solution.py:266
  114.6 18.6 %collective-permute-start.7 = (bf16[8,32,384]{2,1,0:T(8,128)(2,1)S(1)}, bf16[8,32,384]{2,1,0:T(8,128)(2,1)S(1)}, u32[]{:S(2)}, u32[]{:S(2)}) collective-permute-start(bf16[8,32,384]{2,1,0:T(8,128)(2,1)S(1)} %collective-permute-done.6), channel_id=1, source_target_pairs={{41,0},{207,255},{105,64},{15,63},{169,128},{79,127},{233,192},{14... | collective-permute-start | bytes 589832 | tf_op jit(solution)/shard_map/ppermute | solution.py:266
  115.9 3.4 %copy-start.3 = (f32[64,32,1024]{2,1,0:T(8,128)S(1)}, f32[64,32,1024]{2,1,0:T(8,128)}, u32[]{:S(2)}) copy-start(f32[64,32,1024]{2,1,0:T(8,128)} %copy-done.2) | copy-start | bytes 25165828
  (1 other events, 2.2 us)

commit v6 on v5

--- a/solution.py
+++ b/solution.py
@@ -8,7 +8,7 @@
 from jax.sharding import PartitionSpec as P
 
 FAR, RING_TWIN, OWN, TWIN, RING = range(5)
-FAR_CHUNKS = (5, 2)
+FAR_CHUNKS = (6, 1)
 RELAYS = ((5, 1, False), (6, 2, True))
 WHOLE = pl.BlockSpec(memory_space=pltpu.VMEM)
 GRANT = pltpu.CompilerParams(vmem_limit_bytes=16 * 2**20)
@@ -148,23 +148,14 @@
     )(matrices, first, second, part)
 
 
-def last_kernel(start, count, cuts, matrix_ref, part_ref, *refs):
+def last_kernel(start, count, tiles, matrix_ref, part_ref, *refs):
     out_ref, ready_ref, sems = refs[-3:]
     width = ready_ref.shape[0] // count
-    rows, columns = ready_ref.shape[1:]
-    edges = [0, columns // 2, columns] if cuts is None else cuts
-    tiles = list(zip(edges, edges[1:]))
-
-    def far(g, t):
-        lanes = slice(*tiles[t])
-        if cuts is None:
-            return refs[0][pl.ds(g * width, width), :, lanes]
-        if t == 0:
-            return refs[0][...]
-        return refs[2 * t - 1][...] + refs[2 * t][...]
+    rows = ready_ref.shape[1]
 
     def copy(g, t):
-        lanes = pl.ds(tiles[t][0], tiles[t][1] - tiles[t][0])
+        first, last, _ = tiles[t]
+        lanes = pl.ds(first, last - first)
         return pltpu.make_async_copy(
             ready_ref.at[pl.ds(g * width, width), :, lanes],
             out_ref.at[pl.ds((start + g) * width, width), :, lanes],
@@ -172,17 +163,19 @@
         )
 
     def group(g):
-        for t, (first, last) in enumerate(tiles):
-            lanes = slice(first, last)
+        here = pl.ds(g * width, width)
+        for t, (first, last, sources) in enumerate(tiles):
+            far = [refs[i][here, :, first - at : last - at] for i, at in sources]
+            far = far[0] if len(far) == 1 else far[0] + far[1]
             total = jnp.dot(
                 matrix_ref[start + g, FAR],
-                far(g, t).reshape(width * rows, last - first),
+                far.reshape(width * rows, last - first),
                 preferred_element_type=jnp.float32,
             )
-            total = part_ref[pl.ds((start + g) * width, width), :, lanes] + total.reshape(
+            total = part_ref[pl.ds((start + g) * width, width), :, first:last] + total.reshape(
                 width, rows, last - first
             )
-            ready_ref[pl.ds(g * width, width), :, lanes] = jax.nn.gelu(total).astype(jnp.bfloat16)
+            ready_ref[here, :, first:last] = jax.nn.gelu(total).astype(jnp.bfloat16)
             copy(g, t).start()
 
     if count == 1:
@@ -194,22 +187,22 @@
             copy(g, t).wait()
 
 
-def finish(matrices, part, fars, out, start, count, cuts):
+def finish(matrices, part, fars, out, start, count, tiles):
     groups, _, lanes, _ = matrices.shape
     channels, rows, columns = part.shape
     width = channels // groups
     given = [] if out is None else [out]
     whole = pl.BlockSpec(memory_space=pl.ANY)
-    size = count * width * rows * columns
-    return pl.pallas_call(
-        functools.partial(last_kernel, start, count, cuts),
+    size = count * width * rows * sum(last - first for first, last, _ in tiles)
+    return pl.pallas_call(
+        functools.partial(last_kernel, start, count, tiles),
         in_specs=[WHOLE] * (2 + len(fars)) + [whole] * len(given),
         out_specs=whole,
         out_shape=jax.ShapeDtypeStruct(part.shape, jnp.bfloat16),
         input_output_aliases={2 + len(fars): 0} if given else {},
         scratch_shapes=[
             pltpu.VMEM((count * width, rows, columns), jnp.bfloat16),
-            pltpu.SemaphoreType.DMA((3 * count,)),
+            pltpu.SemaphoreType.DMA((len(tiles) * count,)),
         ],
         compiler_params=GRANT,
         cost_estimate=pl.CostEstimate(
@@ -232,8 +225,11 @@
         paths.append([high, strip(x, down_plane, 0, 1), strip(x - 1, down_plane, 3, 1), low])
         for z in range(1, 8) if inner else ():
             low, high = strip(x, z - 1, 3, 1), strip(x, z, 0, 0)
-            paths.append([low, strip(x, z - 1, 2, 1), strip(x, z - 1, 1, 1), high])
+            if z in (RELAYS[0][0], up_plane):
+                paths.append([low, strip(x, z - 1, 2, 1), strip(x, z - 1, 1, 1), high])
             paths.append([high, strip(x, z, 1, 0), strip(x, z, 2, 0), low])
+    if not inner:
+        paths.append([strip(0, 0, 1, 0), strip(1, 0, 1, 1), strip(1, 0, 0, 1), strip(0, 0, 0, 1)])
     return tuple([tuple(path[i : i + 2]) for path in paths] for i in range(3))
 
 
@@ -255,8 +251,8 @@
         start += count
     end = twin[start * width :]
     cuts = [0, 3 * columns // 8, 3 * columns // 4, columns]
-    ends = [lax.ppermute(end[:, :, : cuts[1]], "strip", far_route)]
-    for t, relay in enumerate(RELAYS, 1):
+    ends = []
+    for t, relay in enumerate(RELAYS):
         piece = end[:, :, cuts[t] : cuts[t + 1]]
         hops = relay_hops(devices, *relay)
         relayed = [target for _, target in hops[2]]
@@ -265,18 +261,26 @@
         for hop in hops:
             piece = lax.ppermute(piece, "strip", hop)
         ends.append(piece)
+    final = lax.ppermute(end[:, :, cuts[2] :], "strip", far_route)
     ring_twin = lax.ppermute(ring, "strip", twin_route)
     matrices = banded_matrices(row_kernel, odd, strip_rows)
     own = features
     part = mix(own, mix_weight, channel_bias)
     part = add_pair(matrices, own, OWN, twin, TWIN, part)
     part = add_pair(matrices, ring, RING, ring_twin, RING_TWIN, part)
-    out = None
-    start = 0
-    for far, count in zip(fars, FAR_CHUNKS):
-        out = finish(matrices, part, [far], out, start, count, None)
-        start += count
-    return finish(matrices, part, ends, out, start, 1, cuts)
+    half = columns // 2
+    all_columns = ((0, half, ((0, 0),)), (half, columns, ((0, 0),)))
+    relayed_columns = (
+        (cuts[0], cuts[1], ((0, cuts[0]), (1, cuts[0]))),
+        (cuts[1], cuts[2], ((2, cuts[1]), (3, cuts[1]))),
+    )
+    edge = 7 * columns // 8
+    final_columns = ((cuts[2], edge, ((0, cuts[2]),)), (edge, columns, ((0, cuts[2]),)))
+    first, second = FAR_CHUNKS
+    out = finish(matrices, part, fars[:1], None, 0, first, all_columns)
+    out = finish(matrices, part, ends, out, first + second, 1, relayed_columns)
+    out = finish(matrices, part, fars[1:], out, first, second, all_columns)
+    return finish(matrices, part, [final], out, first + second, 1, final_columns)
 
 
 def solution(mesh):

time: 136 us -> 128 us (0.941)
  the two profiles are of different devices: /device:TPU:0 before, /device:TPU:33 now
where the time goes in v6:
time: 128 us; the launch traced here: 127 us
  waiting for transfers between devices  56.6 us (44%)
  starting transfers between devices  27.1 us (21%)
  Pallas kernels  26.5 us (21%)
  local copies, waits for them, and re-layouts  15.9 us (12%)
    ppermute x1, waiting for transfers between devices, local(): ring = lax.ppermute(features, 'strip', ring_route)  46.5 us
    ppermute x6, starting transfers between devices, local(): piece = lax.ppermute(piece, 'strip', hop)  14.2 us
    pallas_call x2, Pallas kernels, add_pair(): pl.pallas_call(functools.partial(pair_kernel, first_role, second_role), g...  10.9 us
    ppermute x2, waiting for transfers between devices, local(): ends.append(lax.ppermute(piece, 'strip', route))  8.77 us
    reshape x3, local copies, waits for them, and re-layouts, banded_matrices(): jnp.transpose(rows, (0, 3, 1, 2, 4))  7.67 us
    pallas_call x4, Pallas kernels, finish(): pl.pallas_call(functools.partial(last_kernel, start, count, tiles), in_sp...  7.34 us
    pallas_call x1, Pallas kernels, mix(): pl.pallas_call(mix_kernel, grid=(rows // part, 2), in_specs=[pl.BlockSpec...  4.94 us
    unnamed x14, local copies, waits for them, and re-layouts  4.87 us
  transfers between devices with their start and end apart: 14, of which 3 were waited for; matrix products, arithmetic and copies ran while one was open for 9% of the time, Pallas kernels for 20%

profile of v6, /device:TPU:33, one launch (start us, length us, event | category | flops | bytes accessed | tf_op | source)
XLA Modules:
  0.0 127.3 jit_solution(5148359195339161591)
XLA Ops:
  0.0 1.3 %collective-permute-start = (bf16[64,32,1024]{2,1,0:T(8,128)(2,1)}, bf16[64,32,1024]{2,1,0:T(8,128)(2,1)}, u32[]{:S(2)}, u32[]{:S(2)}) collective-permute-start(bf16[64,32,1024]{2,1,0:T(8,128)(2,1)} %first_ref.1), channel_id=1, source_target_pairs={{0,254},{1,3},{2,0},{3,5},{4,2},{5,7},{6,4},{7,9},{8,6},{9,11},{10... | collective-permute-start | bytes 12582920 | tf_op jit(solution)/shard_map/ppermute | solution.py:244
  1.3 1.9 %collective-permute-start.2 = (bf16[64,32,1024]{2,1,0:T(8,128)(2,1)}, bf16[64,32,1024]{2,1,0:T(8,128)(2,1)S(1)}, u32[]{:S(2)}, u32[]{:S(2)}) collective-permute-start(bf16[64,32,1024]{2,1,0:T(8,128)(2,1)} %first_ref.1), channel_id=1, source_target_pairs={{0,1},{1,0},{2,3},{3,2},{4,5},{5,4},{6,7},{7,6},{8,9},{9,8},{10,11... | collective-permute-start | bytes 12582920 | tf_op jit(solution)/shard_map/ppermute | solution.py:245
  3.2 46.5 %collective-permute-done.first_ref = bf16[64,32,1024]{2,1,0:T(8,128)(2,1)} collective-permute-done((bf16[64,32,1024]{2,1,0:T(8,128)(2,1)}, bf16[64,32,1024]{2,1,0:T(8,128)(2,1)}, u32[]{:S(2)}, u32[]{:S(2)}) %collective-permute-start) | collective-permute-done | bytes 4194336 | tf_op jit(solution)/shard_map/ppermute | solution.py:244
  49.8 2.0 %copy-done.2 = bf16[64,32,1024]{2,1,0:T(8,128)(2,1)} copy-done((bf16[64,32,1024]{2,1,0:T(8,128)(2,1)}, bf16[64,32,1024]{2,1,0:T(8,128)(2,1)S(1)}, u32[]{:S(2)}) %copy-start.2) | copy-done | bytes 4194328
  51.8 2.2 %slice.28 = bf16[48,32,1024]{2,1,0:T(8,128)(2,1)} slice(bf16[64,32,1024]{2,1,0:T(8,128)(2,1)S(1)} %collective-permute-done.2.second_ref), slice={[0:48], [0:32], [0:1024]} | slice | bytes 6291456 | tf_op jit(solution)/shard_map/slice | solution.py:249
  55.9 2.8 %reshape.20 = f32[8,8,8,6,32]{4,3,2,1,0:T(8,128)} reshape(f32[8,8,8,192]{3,2,1,0:T(8,128)} %pad_convert_fusion) | data formatting | bytes 786432 | tf_op jit(solution)/shard_map/reshape | solution.py:48
  58.7 3.0 %copy.11 = f32[8,6,8,8,32]{4,3,2,1,0:T(8,128)} copy(f32[8,6,8,8,32]{4,1,3,2,0:T(8,128)} %bitcast.6) | data formatting | bytes 786432 | tf_op jit(solution)/shard_map/reshape | solution.py:48
  61.7 1.9 %reshape.17.rows_ref = f32[8,6,8,256]{3,2,1,0:T(8,128)S(1)} reshape(f32[8,6,8,8,32]{4,3,2,1,0:T(8,128)} %copy.11) | data formatting | bytes 786432 | tf_op jit(solution)/shard_map/reshape | solution.py:48
  64.7 1.3 %collective-permute-start.6 = (bf16[8,32,384]{2,1,0:T(8,128)(2,1)S(1)}, bf16[8,32,384]{2,1,0:T(8,128)(2,1)S(1)}, u32[]{:S(2)}, u32[]{:S(2)}) collective-permute-start(bf16[8,32,384]{2,1,0:T(8,128)(2,1)S(1)} %get-tuple-element.6), channel_id=1, source_target_pairs={{255,239},{0,9},{63,47},{64,73},{127,111},{128,137},{191,175},{192... | collective-permute-start | bytes 589832 | tf_op jit(solution)/shard_map/ppermute | solution.py:262
  66.0 2.1 %collective-permute-start.5 = (bf16[8,32,384]{2,1,0:T(8,128)(2,1)S(1)}, bf16[8,32,384]{2,1,0:T(8,128)(2,1)S(1)}, u32[]{:S(2)}, u32[]{:S(2)}) collective-permute-start(bf16[8,32,384]{2,1,0:T(8,128)(2,1)S(1)} %get-tuple-element.6), channel_id=1, source_target_pairs={{1,2},{3,4},{4,3},{5,6},{6,5},{7,8},{8,7},{9,10},{10,9},{11,12},{1... | collective-permute-start | bytes 589832 | tf_op jit(solution)/shard_map/ppermute | solution.py:260
  68.8 2.2 %copy-done = bf16[64,32,1024]{2,1,0:T(8,128)(2,1)S(1)} copy-done((bf16[64,32,1024]{2,1,0:T(8,128)(2,1)S(1)}, bf16[64,32,1024]{2,1,0:T(8,128)(2,1)}, u32[]{:S(2)}) %copy-start) | copy-done | bytes 4194328
  71.6 4.9 %mix.1.part_ref = f32[64,32,1024]{2,1,0:T(8,128)S(1)} custom-call(f32[64]{0:T(128)S(1)} %copy-done.5, bf16[64,64]{1,0:T(8,128)(2,1)S(1)} %copy-done.4, bf16[64,32,1024]{2,1,0:T(8,128)(2,1)S(1)} %copy-done), custom_call_target="tpu_custom_call" | custom-call | flops 2147483648 | bytes 12582912 | tf_op jit(solution)/shard_map/mix/pallas_call | solution.py:97
  76.7 2.9 %collective-permute-start.4 = (bf16[8,32,1024]{2,1,0:T(8,128)(2,1)S(1)}, bf16[8,32,1024]{2,1,0:T(8,128)(2,1)S(1)}, u32[]{:S(2)}, u32[]{:S(2)}) collective-permute-start(bf16[8,32,1024]{2,1,0:T(8,128)(2,1)S(1)} %slice.25), channel_id=1, source_target_pairs={{0,255},{1,2},{2,1},{3,4},{4,3},{5,6},{6,5},{7,8},{8,7},{9,10},{10... | collective-permute-start | bytes 1572872 | tf_op jit(solution)/shard_map/ppermute | solution.py:250
  79.5 3.3 %banded.1.matrix_ref = bf16[8,5,256,256]{3,2,1,0:T(8,128)(2,1)S(1)} custom-call(s32[1]{0:T(128)} %bitcast.odd_ref, f32[8,6,8,256]{3,2,1,0:T(8,128)S(1)} %reshape.17.rows_ref), custom_call_target="tpu_custom_call" | custom-call | flops 1000000000 | bytes 4000000 | tf_op jit(solution)/shard_map/banded/pallas_call | solution.py:49
  82.9 1.3 collective-permute-done.6
  84.8 8.8 %collective-permute-done.5.refs_0_ = bf16[8,32,384]{2,1,0:T(8,128)(2,1)S(1)} collective-permute-done((bf16[8,32,384]{2,1,0:T(8,128)(2,1)S(1)}, bf16[8,32,384]{2,1,0:T(8,128)(2,1)S(1)}, u32[]{:S(2)}, u32[]{:S(2)}) %collective-permute-start.5) | collective-permute-done | bytes 196640 | tf_op jit(solution)/shard_map/ppermute | solution.py:260
  93.6 10.2 %collective-permute-start.7 = (bf16[8,32,384]{2,1,0:T(8,128)(2,1)S(1)}, bf16[8,32,384]{2,1,0:T(8,128)(2,1)S(1)}, u32[]{:S(2)}, u32[]{:S(2)}) collective-permute-start(bf16[8,32,384]{2,1,0:T(8,128)(2,1)S(1)} %collective-permute-done.6), channel_id=1, source_target_pairs={{239,41},{9,207},{47,105},{73,15},{111,169},{137,79},{175,233},{20... | collective-permute-start | bytes 589832 | tf_op jit(solution)/shard_map/ppermute | solution.py:262
  103.8 3.6 %shard_map.46.part_ref = f32[64,32,1024]{2,1,0:T(8,128)S(1)} custom-call(bf16[8,5,256,256]{3,2,1,0:T(8,128)(2,1)S(1)} %banded.1.matrix_ref, bf16[64,32,1024]{2,1,0:T(8,128)(2,1)S(1)} %copy-done.1, bf16[64,32,1024]{2,1,0:T(8,128)(2,1)S(1)} %copy-done.3, f32[64,32,1024]{2,1,0:T(8,128)S(1)} %mix.1.part_ref), custom_call_target="tpu_custom_call", output_to_operand_aliasing={{}: (3, {})} | custom-call | flops 2147483648 | bytes 8388608 | tf_op jit(solution)/shard_map/pallas_call | solution.py:137
  107.5 1.9 %collective-permute-start.9 = (bf16[8,32,384]{2,1,0:T(8,128)(2,1)S(1)}, bf16[8,32,384]{2,1,0:T(8,128)(2,1)S(1)}, u32[]{:S(2)}, u32[]{:S(2)}) collective-permute-start(bf16[8,32,384]{2,1,0:T(8,128)(2,1)S(1)} %get-tuple-element.5), channel_id=1, source_target_pairs={{1,2},{2,1},{3,4},{4,3},{5,6},{6,5},{7,8},{9,10},{10,9},{11,12},{1... | collective-permute-start | bytes 589832 | tf_op jit(solution)/shard_map/ppermute | solution.py:260
  109.4 1.8 %collective-permute-start.3 = (bf16[8,32,256]{2,1,0:T(8,128)(2,1)S(1)}, bf16[8,32,256]{2,1,0:T(8,128)(2,1)S(1)}, u32[]{:S(2)}, u32[]{:S(2)}) collective-permute-start(bf16[8,32,256]{2,1,0:T(8,128)(2,1)S(1)} %slice.24), channel_id=1, source_target_pairs={{0,255},{1,2},{2,1},{3,4},{4,3},{5,6},{6,5},{7,8},{8,7},{9,10},{10... | collective-permute-start | bytes 393224 | tf_op jit(solution)/shard_map/ppermute | solution.py:264
  112.6 7.3 %shard_map.47.part_ref = f32[64,32,1024]{2,1,0:T(8,128)S(1)} custom-call(bf16[8,5,256,256]{3,2,1,0:T(8,128)(2,1)S(1)} %banded.1.matrix_ref, bf16[64,32,1024]{2,1,0:T(8,128)(2,1)} %collective-permute-done.first_ref, bf16[64,32,1024]{2,1,0:T(8,128)(2,1)} %collective-permute-done.1.second_ref, ...), custom_call_target="tpu_custom_call", output_to_operand_aliasing={{}: (3, {})} | custom-call | flops 2147483648 | bytes 8388608 | tf_op jit(solution)/shard_map/pallas_call | solution.py:137
  119.9 4.0 %shard_map.48.refs_4_ = bf16[64,32,1024]{2,1,0:T(8,128)(2,1)} custom-call(bf16[8,5,256,256]{3,2,1,0:T(8,128)(2,1)S(1)} %banded.1.matrix_ref, f32[64,32,1024]{2,1,0:T(8,128)S(1)} %shard_map.47.part_ref, bf16[48,32,1024]{2,1,0:T(8,128)(2,1)S(1)} %collective-permute-done.13.refs_0_), custom_call_target="tpu_custom_call" | custom-call | flops 805306368 | bytes 6291456 | tf_op jit(solution)/shard_map/pallas_call | solution.py:197
  123.9 1.1 shard_map.49.refs_1_
  125.1 1.3 shard_map.50.refs_1_
  (34 shorter events, 7.3 us)
Async XLA Ops:
  0.0 55.0 %copy-start.6 = (bf16[8,8,8,129]{3,2,1,0:T(8,128)(2,1)S(1)}, bf16[8,8,8,129]{3,2,1,0:T(8,128)(2,1)}, u32[]{:S(2)}) copy-start(bf16[8,8,8,129]{3,2,1,0:T(8,128)(2,1)} %param.5) | copy-start | bytes 396292
  0.0 49.8 %collective-permute-start = (bf16[64,32,1024]{2,1,0:T(8,128)(2,1)}, bf16[64,32,1024]{2,1,0:T(8,128)(2,1)}, u32[]{:S(2)}, u32[]{:S(2)}) collective-permute-start(bf16[64,32,1024]{2,1,0:T(8,128)(2,1)} %first_ref.1), channel_id=1, source_target_pairs={{0,254},{1,3},{2,0},{3,5},{4,2},{5,7},{6,4},{7,9},{8,6},{9,11},{10... | collective-permute-start | bytes 12582920 | tf_op jit(solution)/shard_map/ppermute | solution.py:244
  1.3 48.5 %collective-permute-start.2 = (bf16[64,32,1024]{2,1,0:T(8,128)(2,1)}, bf16[64,32,1024]{2,1,0:T(8,128)(2,1)S(1)}, u32[]{:S(2)}, u32[]{:S(2)}) collective-permute-start(bf16[64,32,1024]{2,1,0:T(8,128)(2,1)} %first_ref.1), channel_id=1, source_target_pairs={{0,1},{1,0},{2,3},{3,2},{4,5},{5,4},{6,7},{7,6},{8,9},{9,8},{10,11... | collective-permute-start | bytes 12582920 | tf_op jit(solution)/shard_map/ppermute | solution.py:245
  49.8 62.1 %collective-permute-start.1 = (bf16[64,32,1024]{2,1,0:T(8,128)(2,1)}, bf16[64,32,1024]{2,1,0:T(8,128)(2,1)}, u32[]{:S(2)}, u32[]{:S(2)}) collective-permute-start(bf16[64,32,1024]{2,1,0:T(8,128)(2,1)} %collective-permute-done.first_ref), channel_id=1, source_target_pairs={{0,1},{1,0},{2,3},{3,2},{4,5},{5,4},{6,7},{7,6},{8,9},{9,8},{10,11... | collective-permute-start | bytes 12582920 | tf_op jit(solution)/shard_map/ppermute | solution.py:265
  49.8 2.0 %copy-start.2 = (bf16[64,32,1024]{2,1,0:T(8,128)(2,1)}, bf16[64,32,1024]{2,1,0:T(8,128)(2,1)S(1)}, u32[]{:S(2)}) copy-start(bf16[64,32,1024]{2,1,0:T(8,128)(2,1)S(1)} %collective-permute-done.2.second_ref) | copy-start | bytes 12582916
  54.1 57.2 %collective-permute-start.13 = (bf16[48,32,1024]{2,1,0:T(8,128)(2,1)}, bf16[48,32,1024]{2,1,0:T(8,128)(2,1)S(1)}, u32[]{:S(2)}, u32[]{:S(2)}) collective-permute-start(bf16[48,32,1024]{2,1,0:T(8,128)(2,1)} %slice.28), channel_id=1, source_target_pairs={{0,255},{1,2},{2,1},{3,4},{4,3},{5,6},{6,5},{7,8},{8,7},{9,10},{10... | collective-permute-start | bytes 9437192 | tf_op jit(solution)/shard_map/ppermute | solution.py:250
  55.9 12.9 %copy-start.4 = (bf16[64,64]{1,0:T(8,128)(2,1)S(1)}, bf16[64,64]{1,0:T(8,128)(2,1)}, u32[]{:S(2)}) copy-start(bf16[64,64]{1,0:T(8,128)(2,1)} %weight_ref.1) | copy-start | bytes 24580
  64.7 19.5 %collective-permute-start.6 = (bf16[8,32,384]{2,1,0:T(8,128)(2,1)S(1)}, bf16[8,32,384]{2,1,0:T(8,128)(2,1)S(1)}, u32[]{:S(2)}, u32[]{:S(2)}) collective-permute-start(bf16[8,32,384]{2,1,0:T(8,128)(2,1)S(1)} %get-tuple-element.6), channel_id=1, source_target_pairs={{255,239},{0,9},{63,47},{64,73},{127,111},{128,137},{191,175},{192... | collective-permute-start | bytes 589832 | tf_op jit(solution)/shard_map/ppermute | solution.py:262
  66.0 27.6 %collective-permute-start.5 = (bf16[8,32,384]{2,1,0:T(8,128)(2,1)S(1)}, bf16[8,32,384]{2,1,0:T(8,128)(2,1)S(1)}, u32[]{:S(2)}, u32[]{:S(2)}) collective-permute-start(bf16[8,32,384]{2,1,0:T(8,128)(2,1)S(1)} %get-tuple-element.6), channel_id=1, source_target_pairs={{1,2},{3,4},{4,3},{5,6},{6,5},{7,8},{8,7},{9,10},{10,9},{11,12},{1... | collective-permute-start | bytes 589832 | tf_op jit(solution)/shard_map/ppermute | solution.py:260
  68.1 8.6 %collective-permute-start.10 = (bf16[8,32,384]{2,1,0:T(8,128)(2,1)S(1)}, bf16[8,32,384]{2,1,0:T(8,128)(2,1)S(1)}, u32[]{:S(2)}, u32[]{:S(2)}) collective-permute-start(bf16[8,32,384]{2,1,0:T(8,128)(2,1)S(1)} %get-tuple-element.5), channel_id=1, source_target_pairs={{255,247},{0,17},{8,10},{16,18},{24,26},{32,34},{39,37},{40,42},{4... | collective-permute-start | bytes 589832 | tf_op jit(solution)/shard_map/ppermute | solution.py:262
  68.8 2.2 %copy-start = (bf16[64,32,1024]{2,1,0:T(8,128)(2,1)S(1)}, bf16[64,32,1024]{2,1,0:T(8,128)(2,1)}, u32[]{:S(2)}) copy-start(bf16[64,32,1024]{2,1,0:T(8,128)(2,1)} %first_ref.1) | copy-start | bytes 12582916
  71.0 0.7 copy-start.5
  71.6 5.0 %copy-start.3 = (bf16[64,32,1024]{2,1,0:T(8,128)(2,1)S(1)}, bf16[64,32,1024]{2,1,0:T(8,128)(2,1)}, u32[]{:S(2)}) copy-start(bf16[64,32,1024]{2,1,0:T(8,128)(2,1)} %copy-done.2) | copy-start | bytes 12582916
  76.6 27.2 %copy-start.1 = (bf16[64,32,1024]{2,1,0:T(8,128)(2,1)S(1)}, bf16[64,32,1024]{2,1,0:T(8,128)(2,1)}, u32[]{:S(2)}) copy-start(bf16[64,32,1024]{2,1,0:T(8,128)(2,1)} %first_ref.1) | copy-start | bytes 12582916
  76.7 48.4 %collective-permute-start.4 = (bf16[8,32,1024]{2,1,0:T(8,128)(2,1)S(1)}, bf16[8,32,1024]{2,1,0:T(8,128)(2,1)S(1)}, u32[]{:S(2)}, u32[]{:S(2)}) collective-permute-start(bf16[8,32,1024]{2,1,0:T(8,128)(2,1)S(1)} %slice.25), channel_id=1, source_target_pairs={{0,255},{1,2},{2,1},{3,4},{4,3},{5,6},{6,5},{7,8},{8,7},{9,10},{10... | collective-permute-start | bytes 1572872 | tf_op jit(solution)/shard_map/ppermute | solution.py:250
  84.2 23.3 %collective-permute-start.11 = (bf16[8,32,384]{2,1,0:T(8,128)(2,1)S(1)}, bf16[8,32,384]{2,1,0:T(8,128)(2,1)S(1)}, u32[]{:S(2)}, u32[]{:S(2)}) collective-permute-start(bf16[8,32,384]{2,1,0:T(8,128)(2,1)S(1)} %collective-permute-done.10), channel_id=1, source_target_pairs={{247,49},{17,215},{10,12},{18,20},{26,28},{34,36},{37,35},{42,44},... | collective-permute-start | bytes 589832 | tf_op jit(solution)/shard_map/ppermute | solution.py:262
  93.6 15.8 %collective-permute-start.7 = (bf16[8,32,384]{2,1,0:T(8,128)(2,1)S(1)}, bf16[8,32,384]{2,1,0:T(8,128)(2,1)S(1)}, u32[]{:S(2)}, u32[]{:S(2)}) collective-permute-start(bf16[8,32,384]{2,1,0:T(8,128)(2,1)S(1)} %collective-permute-done.6), channel_id=1, source_target_pairs={{239,41},{9,207},{47,105},{73,15},{111,169},{137,79},{175,233},{20... | collective-permute-start | bytes 589832 | tf_op jit(solution)/shard_map/ppermute | solution.py:262
  107.5 16.4 %collective-permute-start.9 = (bf16[8,32,384]{2,1,0:T(8,128)(2,1)S(1)}, bf16[8,32,384]{2,1,0:T(8,128)(2,1)S(1)}, u32[]{:S(2)}, u32[]{:S(2)}) collective-permute-start(bf16[8,32,384]{2,1,0:T(8,128)(2,1)S(1)} %get-tuple-element.5), channel_id=1, source_target_pairs={{1,2},{2,1},{3,4},{4,3},{5,6},{6,5},{7,8},{9,10},{10,9},{11,12},{1... | collective-permute-start | bytes 589832 | tf_op jit(solution)/shard_map/ppermute | solution.py:260
  109.4 17.0 %collective-permute-start.3 = (bf16[8,32,256]{2,1,0:T(8,128)(2,1)S(1)}, bf16[8,32,256]{2,1,0:T(8,128)(2,1)S(1)}, u32[]{:S(2)}, u32[]{:S(2)}) collective-permute-start(bf16[8,32,256]{2,1,0:T(8,128)(2,1)S(1)} %slice.24), channel_id=1, source_target_pairs={{0,255},{1,2},{2,1},{3,4},{4,3},{5,6},{6,5},{7,8},{8,7},{9,10},{10... | collective-permute-start | bytes 393224 | tf_op jit(solution)/shard_map/ppermute | solution.py:264
  111.2 12.7 %collective-permute-start.12 = (bf16[8,32,384]{2,1,0:T(8,128)(2,1)S(1)}, bf16[8,32,384]{2,1,0:T(8,128)(2,1)S(1)}, u32[]{:S(2)}, u32[]{:S(2)}) collective-permute-start(bf16[8,32,384]{2,1,0:T(8,128)(2,1)S(1)} %collective-permute-done.11), channel_id=1, source_target_pairs={{49,0},{215,255},{12,7},{20,15},{28,23},{36,31},{35,40},{44,39},{4... | collective-permute-start | bytes 589832 | tf_op jit(solution)/shard_map/ppermute | solution.py:262
  111.9 12.0 %collective-permute-start.8 = (bf16[8,32,384]{2,1,0:T(8,128)(2,1)S(1)}, bf16[8,32,384]{2,1,0:T(8,128)(2,1)S(1)}, u32[]{:S(2)}, u32[]{:S(2)}) collective-permute-start(bf16[8,32,384]{2,1,0:T(8,128)(2,1)S(1)} %collective-permute-done.7), channel_id=1, source_target_pairs={{41,0},{207,255},{105,64},{15,63},{169,128},{79,127},{233,192},{14... | collective-permute-start | bytes 589832 | tf_op jit(solution)/shard_map/ppermute | solution.py:262
